TPU v7x, 32 devices: a whole 2x2x4 slice. The times are simulated.
32 devices in a mesh: kern: 16 (over z, y, x), walk: 2 (over core).
Axes of the slice: x: 2, y: 2, z: 4, core: 2. Of those that a mesh axis runs over, the one named last changes fastest.
Arguments:
- walkers: float32 [8, 2048], P(None, 'walk'), may hold values from -5 to 5
- centers: float32 [8, 32768], P(None, 'kern'), may hold values from -5 to 5
- sigmas: float32 [8, 32768], P(None, 'kern'), may hold values from 0.6 to 1.5
- heights: float32 [32768], P('kern'), may hold values from 0.2 to 2
- kernel_live: int32 [16], P('kern'), may hold values from 512 to 2048, as said below
- merge_target: int32 [2048], P('walk'), may hold values from 0 to 32767, as said below
- new_sigma: float32 [8], replicated, may hold values from 0.2 to 0.6
- norm_old: float32 [1], replicated, may hold values from 0.003 to 0.03
Outputs:
- bias: float32 [2048], P('walk')
- force: float32 [8, 2048], P(None, 'walk')
- new_heights: float32 [32768], P('kern')
- new_centers: float32 [8, 32768], P(None, 'kern')
- new_sigmas: float32 [8, 32768], P(None, 'kern')
- log_norm: float32 [1], replicated
Inputs may be any that keep to these rules, and one draw needn't show every extreme that they name: `kernel_live`: slots from this number up are empty; some shard is full in every draw. `merge_target`: each entry is shard * 2048 + slot with slot below that shard's kernel_live; among the 1024 walkers of one index of walk at most 128 target one shard, every shard is targeted, and some shard receives exactly 128 in every block.
All inputs are finite; a program needn't handle non-finite values.
Results may differ from a plain program's by a relative error of at most 0.0003.
Values sent between devices are 32-bit elements; how exact they have to be, the bound alone decides.
A program may use at most 64 MiB of HBM per device.

v0:
```python
import functools
import math

import jax
import jax.numpy as jnp
from jax import lax
from jax.experimental import pallas as pl
from jax.experimental.pallas import tpu as pltpu
from jax.sharding import PartitionSpec as P

PREFACTOR = 0.9
EPSILON = 0.01
RATE = 0.25
LANES = 128
LOG2E = math.log2(math.e)
MESH = pl.DeviceIdType.MESH
F32 = jnp.float32
BF16 = jnp.bfloat16
VMEM = pl.BlockSpec(memory_space=pltpu.VMEM)
HBM = pl.BlockSpec(memory_space=pltpu.HBM)


def split(x):
    high = x.astype(BF16).astype(F32)
    rest = x - high
    middle = rest.astype(BF16).astype(F32)
    low = (rest - middle).astype(BF16).astype(F32)
    return high, middle, low


def row_of(parts, width):
    row = lax.broadcasted_iota(jnp.int32, (8, width), 0)
    block = jnp.zeros((8, width), F32)
    for index, part in enumerate(parts):
        block = jnp.where(row == index, part, block)
    return block


def farthest_first(count):
    return sorted(range(count), key=lambda step: -min(step, count - step))


def sums_kernel(kern_count, walk_count, groups, capacity,
                walkers_hbm, target_hbm, centers_hbm, sigmas_hbm, heights_hbm, live_hbm, norm_hbm,
                share_ref, density_ref, packed_ref, packed_slot_ref, packed_density_ref, norm_out_ref,
                walkers_ref, target_ref, centers_ref, sigmas_ref, heights_ref, live_ref, norm_ref, load_sem,
                walker_feat, kernel_feat, kernel_mom, sums, own, got, mine, shared, far,
                far_walkers, far_targets, table,
                send_a, recv_a, send_b, recv_b, send_c, recv_c, send_w, recv_w, send_t, recv_t):
    loads = [
        pltpu.make_async_copy(source, target, load_sem.at[index])
        for index, (source, target) in enumerate(
            [
                (walkers_hbm, walkers_ref),
                (centers_hbm, centers_ref),
                (sigmas_hbm, sigmas_ref),
                (heights_hbm, heights_ref),
                (live_hbm, live_ref),
                (norm_hbm, norm_ref),
                (target_hbm, target_ref),
            ]
        )
    ]
    for load in loads:
        load.start()
    dims, walk_len = walkers_ref.shape
    shard_len = centers_ref.shape[1]
    per = dims // groups
    chunks = kern_count // groups
    me = lax.axis_index("kern")
    walk = lax.axis_index("walk")
    my_chunk = me // groups
    my_group = lax.rem(me, groups)

    def peer(step):
        return lax.rem(me + step, kern_count)

    def other(step):
        return lax.rem(walk + step, walk_count)

    def far_kern(index):
        return index * groups + my_group

    barrier = pltpu.get_barrier_semaphore()

    def greet(step, carry):
        pl.semaphore_signal(barrier, inc=1, device_id=(peer(step), walk), device_id_type=MESH)
        return carry

    lax.fori_loop(1, kern_count, greet, 0)
    for step in range(1, walk_count):
        def greet_far(index, carry):
            pl.semaphore_signal(
                barrier, inc=1, device_id=(far_kern(index), other(step)), device_id_type=MESH
            )
            return carry

        lax.fori_loop(0, chunks, greet_far, 0)

    for load in loads:
        load.wait()
    norm = norm_ref[0]
    norm_out_ref[...] = jnp.full((1, 1), norm, F32)
    walkers = walkers_ref[...]
    sq_h, sq_m, sq_l = split(walkers * walkers)
    wk_h, wk_m, wk_l = split(walkers)
    h, m, l = [sq_h, wk_h], [sq_m, wk_m], [sq_l, wk_l]
    one = jnp.ones((1, walk_len), F32)
    pad = jnp.zeros((LANES - 12 * dims - 8, walk_len), F32)
    stacked = jnp.concatenate(h + m + h + m + l + h + [row_of([one] * 3, walk_len), pad], 0)
    stacked = stacked.astype(BF16)
    width = 2 * LANES
    quarters = walk_len // width
    for quarter in range(quarters):
        walker_feat[quarter] = stacked[:, quarter * width : (quarter + 1) * width]

    centers = centers_ref[...]
    sigmas = sigmas_ref[...]
    inverse_var = 1.0 / (sigmas * sigmas)
    scaled = centers * inverse_var
    constant = jnp.log(heights_ref[...]) - 0.5 * jnp.sum(centers * scaled, 0, keepdims=True)
    k_sq = split((-0.5 * LOG2E) * inverse_var)
    k_lin = split(LOG2E * scaled)
    con = row_of(split(LOG2E * constant), shard_len)
    h, m, l = [[k_sq[i], k_lin[i]] for i in range(3)]
    pad = jnp.zeros((LANES - 12 * dims - 8, shard_len), F32)
    kernel_feat[...] = jnp.concatenate(h + h + m + m + h + l + [con, pad], 0).T.astype(BF16)

    live = live_ref[0]
    alive = (lax.broadcasted_iota(jnp.int32, (8, shard_len), 1) < live).astype(F32)
    mom_a = split(inverse_var * alive)
    mom_c = split(scaled * alive)
    pad = jnp.zeros((8, shard_len), F32)
    rows = [mom_a[0], mom_c[0], mom_a[1], mom_c[1], mom_a[2], mom_c[2], row_of([alive], shard_len), pad]
    kernel_mom[...] = jnp.concatenate(rows, 0).astype(BF16)

    live_row = jnp.full((1, LANES), live, jnp.int32).astype(F32)
    for unit in range(kern_count):
        chunk, group = unit // groups, unit % groups
        own[unit] = walkers[group * per : (group + 1) * per, chunk * LANES : (chunk + 1) * LANES]

    units = kern_count // quarters
    block = min(512, shard_len)

    def copy_a(target, source):
        return pltpu.make_async_remote_copy(
            src_ref=sums.at[target], dst_ref=got.at[source],
            send_sem=send_a.at[target], recv_sem=recv_a.at[source],
            device_id=(target, walk), device_id_type=MESH,
        )

    def compute(step):
        quarter = lax.rem(me // units + step, quarters)
        feat = walker_feat[quarter]
        total = None
        for index in range(shard_len // block):
            part = slice(index * block, (index + 1) * block)
            e = jnp.exp2(jnp.dot(kernel_feat[part, :], feat, preferred_element_type=F32))
            high = e.astype(BF16)
            low = (e - high.astype(F32)).astype(BF16)
            moms = kernel_mom[:, part]
            add = jnp.dot(moms, high, preferred_element_type=F32) + jnp.dot(
                moms, low, preferred_element_type=F32
            )
            total = add if total is None else total + add
        moments = total
        a_sum = moments[0:dims] + moments[2 * dims : 3 * dims] + moments[4 * dims : 5 * dims]
        c_sum = moments[dims : 2 * dims] + moments[3 * dims : 4 * dims] + moments[5 * dims : 6 * dims]
        density = moments[6 * dims : 6 * dims + 1]
        for chunk in range(2):
            part = slice(chunk * LANES, (chunk + 1) * LANES)
            for group in range(groups):
                unit = quarter * units + chunk * groups + group
                rows = slice(group * per, (group + 1) * per)
                sums[unit, 0:per, :] = a_sum[rows, part]
                sums[unit, per : 2 * per, :] = c_sum[rows, part]
                sums[unit, 2 * per : 2 * per + 1, :] = density[:, part]
                sums[unit, 2 * per + 1 : 2 * per + 2, :] = live_row

    def send(step):
        quarter = lax.rem(me // units + step, quarters)

        def start_a(index, carry):
            copy_a(quarter * units + lax.rem(me + index, units), me).start()
            return carry

        lax.fori_loop(0 if step else 1, units, start_a, 0)

    def copy_w(step, source):
        return (
            pltpu.make_async_remote_copy(
                src_ref=walkers_ref, dst_ref=far_walkers.at[source],
                send_sem=send_w.at[step], recv_sem=recv_w.at[source],
                device_id=(me, other(step)), device_id_type=MESH,
            ),
            pltpu.make_async_remote_copy(
                src_ref=target_ref, dst_ref=far_targets.at[source],
                send_sem=send_t.at[step], recv_sem=recv_t.at[source],
                device_id=(me, other(step)), device_id_type=MESH,
            ),
        )

    order = farthest_first(quarters)
    for position, step in enumerate(order):
        compute(step)
        if position == 1:
            pl.semaphore_wait(barrier, kern_count - 1 + (walk_count - 1) * chunks)
            send(order[0])
            for far_step in range(1, walk_count):
                for copy in copy_w(far_step, walk):
                    copy.start()
        if position >= 1:
            send(step)

    got[me] = sums[me]
    def wait_a(step, carry):
        copy_a(peer(step), peer(step)).wait_recv()
        return carry

    lax.fori_loop(1, kern_count, wait_a, 0)
    total = got[0]
    for source in range(1, kern_count):
        total = total + got[source]

    live_total = total[2 * per + 1 : 2 * per + 2]
    density = total[2 * per : 2 * per + 1] / live_total
    grad = (-own[me] * total[0:per] + total[per : 2 * per]) / live_total
    ratio = density / norm + EPSILON
    force = -PREFACTOR * grad / (norm * ratio)
    mine[0:1, :] = density
    mine[1 : per + 1, :] = force

    def copy_b(target, source):
        return pltpu.make_async_remote_copy(
            src_ref=mine, dst_ref=shared.at[source],
            send_sem=send_b.at[target], recv_sem=recv_b.at[source],
            device_id=(target, walk), device_id_type=MESH,
        )

    def copy_c(step, index, chunk, source):
        return pltpu.make_async_remote_copy(
            src_ref=mine, dst_ref=far.at[source, chunk],
            send_sem=send_c.at[step, index], recv_sem=recv_c.at[source, chunk],
            device_id=(far_kern(index), other(step)), device_id_type=MESH,
        )

    def start_b(step, carry):
        copy_b(peer(step), me).start()
        return carry

    for step in range(1, walk_count):
        def start_c(index, carry):
            copy_c(step, lax.rem(my_chunk + index, chunks), my_chunk, walk).start()
            return carry

        half = chunks // 2
        lax.fori_loop(half, chunks, start_c, 0)
        lax.fori_loop(0, half, start_c, 0)
    lax.fori_loop(kern_count // 2, kern_count, start_b, 0)
    lax.fori_loop(1, kern_count // 2, start_b, 0)

    shared[me, 0:1, :] = density
    shared[me, 1 : per + 1, :] = force

    far_walkers[walk] = walkers
    far_targets[walk] = target_ref[...]
    for step in range(1, walk_count):
        for copy in copy_w(step, other(step)):
            copy.wait_recv()
    targets = [far_targets[index] for index in range(walk_count)]
    if walk_count % 8:
        targets.append(jnp.full((8 - walk_count % 8, walk_len), -1, jnp.int32))
    local = jnp.concatenate(targets, 0) - me * shard_len
    owned = (local >= 0) & (local < shard_len)
    before = lax.broadcasted_iota(jnp.int32, (walk_len, walk_len), 0) < lax.broadcasted_iota(
        jnp.int32, (walk_len, walk_len), 1
    )
    place = jnp.dot(
        jnp.where(owned, 1.0, 0.0).astype(BF16),
        jnp.where(before, 1.0, 0.0).astype(BF16),
        preferred_element_type=F32,
    )
    place = jnp.where(owned, place, -1.0)
    slot = jnp.where(owned, (local + 1).astype(F32), 0.0)
    want = lax.broadcasted_iota(jnp.int32, (capacity, walk_len), 0).astype(F32)

    def pack(feat, index):
        return lax.dot_general(
            feat.astype(BF16), table[index], (((1,), (1,)), ((), ())), preferred_element_type=F32
        )

    for index in range(walk_count):
        table[index] = jnp.where(want == place[index : index + 1], 1.0, 0.0).astype(BF16)
        high, middle, low = split(far_walkers[index])
        slot_rows = row_of(split(slot[index : index + 1]), walk_len)
        packed = pack(jnp.concatenate([high, middle, low, slot_rows], 0), index)
        packed_ref[index] = packed[0:dims] + (packed[dims : 2 * dims] + packed[2 * dims : 3 * dims])
        at = 3 * dims
        packed_slot_ref[index] = packed[at : at + 1] + packed[at + 1 : at + 2] + packed[at + 2 : at + 3] - 1.0

    def wait_b(step, carry):
        copy_b(peer(step), peer(step)).wait_recv()
        return carry

    lax.fori_loop(1, kern_count, wait_b, 0)
    for chunk in range(chunks):
        far[walk, chunk] = shared[chunk * groups]
    share_ref[...] = shared[...]
    for step in range(1, walk_count):
        def wait_c(index, carry):
            copy_c(step, index, index, other(step)).wait_recv()
            return carry

        lax.fori_loop(0, chunks, wait_c, 0)
    for index in range(walk_count):
        whole = jnp.concatenate([far[index, chunk][0:1, :] for chunk in range(chunks)], 1)
        density_ref[index] = whole
        packed = pack(row_of(split(whole), walk_len), index)
        packed_density_ref[index] = packed[0:1] + packed[1:2] + packed[2:3]

    def wait_sends(step, carry):
        copy_a(peer(step), me).wait_send()
        copy_b(peer(step), me).wait_send()
        return carry

    lax.fori_loop(1, kern_count, wait_sends, 0)
    for step in range(1, walk_count):
        def wait_send_c(index, carry):
            copy_c(step, index, my_chunk, walk).wait_send()
            return carry

        lax.fori_loop(0, chunks, wait_send_c, 0)
        for copy in copy_w(step, walk):
            copy.wait_send()


def merge_kernel(groups, share_ref, density_ref, packed_ref, packed_slot_ref, packed_density_ref,
                 centers_ref, sigmas_ref, heights_ref, new_sigma_ref, norm_ref,
                 bias_ref, force_ref, new_heights_ref, new_centers_ref, new_sigmas_ref, log_norm_ref):
    dims, shard_len = centers_ref.shape
    walk_count, _, walk_len = density_ref.shape
    capacity = packed_ref.shape[2]
    per = dims // groups
    chunks = walk_len // LANES
    norm = norm_ref[...]

    def biased(density):
        return PREFACTOR * jnp.log(density / norm + EPSILON)

    for chunk in range(chunks):
        part = slice(chunk * LANES, (chunk + 1) * LANES)
        bias_ref[:, part] = biased(share_ref[chunk * groups][0:1, :])
        for group in range(groups):
            force_ref[group * per : (group + 1) * per, part] = share_ref[chunk * groups + group][1 : per + 1, :]

    density_sum = jnp.zeros((1, 1), F32)
    for index in range(walk_count):
        density_sum = density_sum + jnp.sum(density_ref[index], 1, keepdims=True)
    log_norm_ref[...] = jnp.log((1.0 - RATE) * norm + RATE * density_sum / (walk_len * walk_count))

    slots = lax.broadcasted_iota(jnp.int32, (shard_len, capacity), 0).astype(F32)
    sums = None
    for index in range(walk_count):
        weight = jnp.exp(biased(packed_density_ref[index]))
        walkers = packed_ref[index]
        lin = split(weight * walkers)
        sq = split(weight * (walkers * walkers))
        last = row_of(split(weight), capacity)
        pad = jnp.zeros((8, capacity), F32)
        feat = jnp.concatenate([lin[0], sq[0], lin[1], sq[1], lin[2], sq[2], last, pad], 0).astype(BF16)
        placing = jnp.where(slots == packed_slot_ref[index], 1.0, 0.0).astype(BF16)
        add = lax.dot_general(feat, placing, (((1,), (1,)), ((), ())), preferred_element_type=F32)
        sums = add if sums is None else sums + add

    first = sums[0:dims] + (sums[2 * dims : 3 * dims] + sums[4 * dims : 5 * dims])
    second = sums[dims : 2 * dims] + (sums[3 * dims : 4 * dims] + sums[5 * dims : 6 * dims])
    at = 6 * dims
    gain = sums[at : at + 1] + (sums[at + 1 : at + 2] + sums[at + 2 : at + 3])
    row = lax.broadcasted_iota(jnp.int32, (dims, dims), 0)
    column = lax.broadcasted_iota(jnp.int32, (dims, dims), 1)
    new_sigma = jnp.sum(jnp.where(row == column, new_sigma_ref[...], 0.0), 1, keepdims=True)
    centers = centers_ref[...]
    sigmas = sigmas_ref[...]
    heights = heights_ref[...]
    shift = first - centers * gain
    spread = second - 2.0 * centers * first + centers * centers * gain + new_sigma * new_sigma * gain
    new_heights = heights + gain
    delta = shift / new_heights
    new_heights_ref[...] = new_heights
    new_centers_ref[...] = centers + delta
    new_sigmas_ref[...] = jnp.sqrt((heights * sigmas * sigmas + spread) / new_heights - delta * delta)


def per_device(walkers, centers, sigmas, heights, kernel_live, merge_target, new_sigma, norm_old):
    dims, walk_len = walkers.shape
    shard_len = centers.shape[1]
    kern_count = lax.axis_size("kern")
    walk_count = lax.axis_size("walk")
    chunks = walk_len // LANES
    groups = kern_count // chunks
    per = dims // groups
    capacity = 2 * walk_len // kern_count
    height_row = heights.reshape(1, shard_len)

    dma = pltpu.SemaphoreType.DMA
    share, density, packed, packed_slot, packed_density, norm_row = pl.pallas_call(
        functools.partial(sums_kernel, kern_count, walk_count, groups, capacity),
        out_shape=(
            jax.ShapeDtypeStruct((kern_count, per + 1, LANES), F32),
            jax.ShapeDtypeStruct((walk_count, 1, walk_len), F32),
            jax.ShapeDtypeStruct((walk_count, dims, capacity), F32),
            jax.ShapeDtypeStruct((walk_count, 1, capacity), F32),
            jax.ShapeDtypeStruct((walk_count, 1, capacity), F32),
            jax.ShapeDtypeStruct((1, 1), F32),
        ),
        in_specs=[HBM] * 7,
        out_specs=(VMEM,) * 6,
        scratch_shapes=[
            pltpu.VMEM((dims, walk_len), F32),
            pltpu.VMEM((1, walk_len), jnp.int32),
            pltpu.VMEM((dims, shard_len), F32),
            pltpu.VMEM((dims, shard_len), F32),
            pltpu.VMEM((1, shard_len), F32),
            pltpu.SMEM((1,), jnp.int32),
            pltpu.SMEM((1,), F32),
            dma((7,)),
            pltpu.VMEM((walk_len // (2 * LANES), LANES, 2 * LANES), BF16),
            pltpu.VMEM((shard_len, LANES), BF16),
            pltpu.VMEM((6 * dims + 16, shard_len), BF16),
            pltpu.VMEM((kern_count, 2 * per + 2, LANES), F32),
            pltpu.VMEM((kern_count, per, LANES), F32),
            pltpu.VMEM((kern_count, 2 * per + 2, LANES), F32),
            pltpu.VMEM((per + 1, LANES), F32),
            pltpu.VMEM((kern_count, per + 1, LANES), F32),
            pltpu.VMEM((walk_count, chunks, per + 1, LANES), F32),
            pltpu.VMEM((walk_count, dims, walk_len), F32),
            pltpu.VMEM((walk_count, 1, walk_len), jnp.int32),
            pltpu.VMEM((walk_count, capacity, walk_len), BF16),
            dma((kern_count,)), dma((kern_count,)),
            dma((kern_count,)), dma((kern_count,)),
            dma((walk_count, chunks)), dma((walk_count, chunks)),
            dma((walk_count,)), dma((walk_count,)),
            dma((walk_count,)), dma((walk_count,)),
        ],
        compiler_params=pltpu.CompilerParams(collective_id=0, has_side_effects=True),
        name="sums",
    )(walkers, merge_target.reshape(1, walk_len), centers, sigmas, height_row, kernel_live, norm_old)

    bias, force, new_heights, new_centers, new_sigmas, log_norm = pl.pallas_call(
        functools.partial(merge_kernel, groups),
        out_shape=(
            jax.ShapeDtypeStruct((1, walk_len), F32),
            jax.ShapeDtypeStruct((dims, walk_len), F32),
            jax.ShapeDtypeStruct((1, shard_len), F32),
            jax.ShapeDtypeStruct((dims, shard_len), F32),
            jax.ShapeDtypeStruct((dims, shard_len), F32),
            jax.ShapeDtypeStruct((1, 1), F32),
        ),
        in_specs=[VMEM] * 10,
        out_specs=(VMEM,) * 6,
        name="merge",
    )(share, density, packed, packed_slot, packed_density, centers, sigmas, height_row, new_sigma.reshape(1, dims), norm_row)
    return (bias.reshape(walk_len), force, new_heights.reshape(shard_len), new_centers, new_sigmas, log_norm.reshape(1))


def solution(mesh):
    in_specs = (
        P(None, "walk"),
        P(None, "kern"),
        P(None, "kern"),
        P("kern"),
        P("kern"),
        P("walk"),
        P(),
        P(),
    )
    out_specs = (P("walk"), P(None, "walk"), P("kern"), P(None, "kern"), P(None, "kern"), P())
    return jax.shard_map(
        per_device, mesh=mesh, in_specs=in_specs, out_specs=out_specs, check_vma=False
    )
```

profile of v0, /device:TPU:0, one launch (start us, length us, event | category | flops | bytes accessed | tf_op | source)
XLA Modules:
  0.0 24.1 jit_solution(1707173345865816987)
XLA Ops:
  1.9 19.4 %sums.1 = (f32[16,5,128]{2,1,0:T(8,128)}, f32[2,1,1024]{2,1,0:T(1,128)}, f32[2,8,128]{2,1,0:T(8,128)}, f32[2,1,128]{2,1,0:T(1,128)}, f32[2,1,128]{2,1,0:T(1,128)}, /*index=5*/f32[1,1]{1,0:T(1,128)}) custom-call(f32[8,1024]{1,0:T(8,128)} %walkers_hbm.1, s32[1,1024]{1,0:T(1,128)} %bitcast.8, f32[8,2048]{1,0:T(8,128)} %centers_ref.1, f32[8,2048]{1,0:T(8,128)} %sigmas_ref.1, ...), custom_call_target="tpu_custom_call" | custom-call | tf_op jit(solution)/shard_map/sums/pallas_call | solution.py:406
  21.3 2.8 %merge.1 = (f32[1,1024]{1,0:T(1,128)}, f32[8,1024]{1,0:T(8,128)}, f32[1,2048]{1,0:T(1,128)}, f32[8,2048]{1,0:T(8,128)}, f32[8,2048]{1,0:T(8,128)}, /*index=5*/f32[1,1]{1,0:T(1,128)}) custom-call(f32[16,5,128]{2,1,0:T(8,128)} %get-tuple-element.18.share_ref, f32[2,1,1024]{2,1,0:T(1,128)} %get-tuple-element.19.density_ref, ...), custom_call_target="tpu_custom_call" | custom-call | tf_op jit(solution)/shard_map/merge/pallas_call | solution.py:449
where the time goes:
time: 24.3 us; the launch traced here: 24.1 us
  Pallas kernels  22.2 us (91%)
  between operations  1.93 us (8%)
    pallas_call x1, Pallas kernels, per_device(): pl.pallas_call(functools.partial(sums_kernel, kern_count, walk_count, gro...  19.4 us
    pallas_call x1, Pallas kernels, per_device(): pl.pallas_call(functools.partial(merge_kernel, groups), out_shape=(jax.Sh...  2.78 us

commit v1 on v0

--- a/solution.py
+++ b/solution.py
@@ -18,6 +18,7 @@
 BF16 = jnp.bfloat16
 VMEM = pl.BlockSpec(memory_space=pltpu.VMEM)
 HBM = pl.BlockSpec(memory_space=pltpu.HBM)
+LIMIT = 24 << 20
 
 
 def split(x):
@@ -41,11 +42,11 @@
 
 
 def sums_kernel(kern_count, walk_count, groups, capacity,
-                walkers_hbm, target_hbm, centers_hbm, sigmas_hbm, heights_hbm, live_hbm, norm_hbm,
-                share_ref, density_ref, packed_ref, packed_slot_ref, packed_density_ref, norm_out_ref,
-                walkers_ref, target_ref, centers_ref, sigmas_ref, heights_ref, live_ref, norm_ref, load_sem,
+                walkers_hbm, target_hbm, centers_hbm, sigmas_hbm, heights_hbm, live_hbm, norm_hbm, new_sigma_hbm,
+                bias_ref, force_ref, new_heights_ref, new_centers_ref, new_sigmas_ref, log_norm_ref,
+                walkers_ref, target_ref, centers_ref, sigmas_ref, heights_ref, live_ref, norm_ref, new_sigma_ref, load_sem,
                 walker_feat, kernel_feat, kernel_mom, sums, own, got, mine, shared, far,
-                far_walkers, far_targets, table,
+                far_walkers, far_targets, table, placing,
                 send_a, recv_a, send_b, recv_b, send_c, recv_c, send_w, recv_w, send_t, recv_t):
     loads = [
         pltpu.make_async_copy(source, target, load_sem.at[index])
@@ -58,6 +59,7 @@
                 (live_hbm, live_ref),
                 (norm_hbm, norm_ref),
                 (target_hbm, target_ref),
+                (new_sigma_hbm, new_sigma_ref),
             ]
         )
     ]
@@ -72,6 +74,9 @@
     my_chunk = me // groups
     my_group = lax.rem(me, groups)
 
+    def biased(density):
+        return PREFACTOR * jnp.log(density / norm + EPSILON)
+
     def peer(step):
         return lax.rem(me + step, kern_count)
 
@@ -100,7 +105,6 @@
     for load in loads:
         load.wait()
     norm = norm_ref[0]
-    norm_out_ref[...] = jnp.full((1, 1), norm, F32)
     walkers = walkers_ref[...]
     sq_h, sq_m, sq_l = split(walkers * walkers)
     wk_h, wk_m, wk_l = split(walkers)
@@ -289,14 +293,17 @@
             feat.astype(BF16), table[index], (((1,), (1,)), ((), ())), preferred_element_type=F32
         )
 
+    slots = lax.broadcasted_iota(jnp.int32, (shard_len, capacity), 0).astype(F32)
+    packed_walkers = []
     for index in range(walk_count):
         table[index] = jnp.where(want == place[index : index + 1], 1.0, 0.0).astype(BF16)
         high, middle, low = split(far_walkers[index])
         slot_rows = row_of(split(slot[index : index + 1]), walk_len)
         packed = pack(jnp.concatenate([high, middle, low, slot_rows], 0), index)
-        packed_ref[index] = packed[0:dims] + (packed[dims : 2 * dims] + packed[2 * dims : 3 * dims])
+        packed_walkers.append(packed[0:dims] + (packed[dims : 2 * dims] + packed[2 * dims : 3 * dims]))
         at = 3 * dims
-        packed_slot_ref[index] = packed[at : at + 1] + packed[at + 1 : at + 2] + packed[at + 2 : at + 3] - 1.0
+        packed_slot = packed[at : at + 1] + packed[at + 1 : at + 2] + packed[at + 2 : at + 3] - 1.0
+        placing[index] = jnp.where(slots == packed_slot, 1.0, 0.0).astype(BF16)
 
     def wait_b(step, carry):
         copy_b(peer(step), peer(step)).wait_recv()
@@ -305,77 +312,37 @@
     lax.fori_loop(1, kern_count, wait_b, 0)
     for chunk in range(chunks):
         far[walk, chunk] = shared[chunk * groups]
-    share_ref[...] = shared[...]
+    for chunk in range(chunks):
+        part = slice(chunk * LANES, (chunk + 1) * LANES)
+        bias_ref[:, part] = biased(shared[chunk * groups][0:1, :])
+        for group in range(groups):
+            force_ref[group * per : (group + 1) * per, part] = shared[chunk * groups + group][1 : per + 1, :]
     for step in range(1, walk_count):
         def wait_c(index, carry):
             copy_c(step, index, index, other(step)).wait_recv()
             return carry
 
         lax.fori_loop(0, chunks, wait_c, 0)
+    density_sum = jnp.zeros((1, 1), F32)
+    merged = None
     for index in range(walk_count):
         whole = jnp.concatenate([far[index, chunk][0:1, :] for chunk in range(chunks)], 1)
-        density_ref[index] = whole
+        density_sum = density_sum + jnp.sum(whole, 1, keepdims=True)
         packed = pack(row_of(split(whole), walk_len), index)
-        packed_density_ref[index] = packed[0:1] + packed[1:2] + packed[2:3]
-
-    def wait_sends(step, carry):
-        copy_a(peer(step), me).wait_send()
-        copy_b(peer(step), me).wait_send()
-        return carry
-
-    lax.fori_loop(1, kern_count, wait_sends, 0)
-    for step in range(1, walk_count):
-        def wait_send_c(index, carry):
-            copy_c(step, index, my_chunk, walk).wait_send()
-            return carry
-
-        lax.fori_loop(0, chunks, wait_send_c, 0)
-        for copy in copy_w(step, walk):
-            copy.wait_send()
-
-
-def merge_kernel(groups, share_ref, density_ref, packed_ref, packed_slot_ref, packed_density_ref,
-                 centers_ref, sigmas_ref, heights_ref, new_sigma_ref, norm_ref,
-                 bias_ref, force_ref, new_heights_ref, new_centers_ref, new_sigmas_ref, log_norm_ref):
-    dims, shard_len = centers_ref.shape
-    walk_count, _, walk_len = density_ref.shape
-    capacity = packed_ref.shape[2]
-    per = dims // groups
-    chunks = walk_len // LANES
-    norm = norm_ref[...]
-
-    def biased(density):
-        return PREFACTOR * jnp.log(density / norm + EPSILON)
-
-    for chunk in range(chunks):
-        part = slice(chunk * LANES, (chunk + 1) * LANES)
-        bias_ref[:, part] = biased(share_ref[chunk * groups][0:1, :])
-        for group in range(groups):
-            force_ref[group * per : (group + 1) * per, part] = share_ref[chunk * groups + group][1 : per + 1, :]
-
-    density_sum = jnp.zeros((1, 1), F32)
-    for index in range(walk_count):
-        density_sum = density_sum + jnp.sum(density_ref[index], 1, keepdims=True)
-    log_norm_ref[...] = jnp.log((1.0 - RATE) * norm + RATE * density_sum / (walk_len * walk_count))
-
-    slots = lax.broadcasted_iota(jnp.int32, (shard_len, capacity), 0).astype(F32)
-    sums = None
-    for index in range(walk_count):
-        weight = jnp.exp(biased(packed_density_ref[index]))
-        walkers = packed_ref[index]
-        lin = split(weight * walkers)
-        sq = split(weight * (walkers * walkers))
+        weight = jnp.exp(biased(packed[0:1] + packed[1:2] + packed[2:3]))
+        lin = split(weight * packed_walkers[index])
+        sq = split(weight * (packed_walkers[index] * packed_walkers[index]))
         last = row_of(split(weight), capacity)
         pad = jnp.zeros((8, capacity), F32)
         feat = jnp.concatenate([lin[0], sq[0], lin[1], sq[1], lin[2], sq[2], last, pad], 0).astype(BF16)
-        placing = jnp.where(slots == packed_slot_ref[index], 1.0, 0.0).astype(BF16)
-        add = lax.dot_general(feat, placing, (((1,), (1,)), ((), ())), preferred_element_type=F32)
-        sums = add if sums is None else sums + add
-
-    first = sums[0:dims] + (sums[2 * dims : 3 * dims] + sums[4 * dims : 5 * dims])
-    second = sums[dims : 2 * dims] + (sums[3 * dims : 4 * dims] + sums[5 * dims : 6 * dims])
+        add = lax.dot_general(feat, placing[index], (((1,), (1,)), ((), ())), preferred_element_type=F32)
+        merged = add if merged is None else merged + add
+    log_norm_ref[...] = jnp.log((1.0 - RATE) * norm + RATE * density_sum / (walk_len * walk_count))
+
+    first = merged[0:dims] + (merged[2 * dims : 3 * dims] + merged[4 * dims : 5 * dims])
+    second = merged[dims : 2 * dims] + (merged[3 * dims : 4 * dims] + merged[5 * dims : 6 * dims])
     at = 6 * dims
-    gain = sums[at : at + 1] + (sums[at + 1 : at + 2] + sums[at + 2 : at + 3])
+    gain = merged[at : at + 1] + (merged[at + 1 : at + 2] + merged[at + 2 : at + 3])
     row = lax.broadcasted_iota(jnp.int32, (dims, dims), 0)
     column = lax.broadcasted_iota(jnp.int32, (dims, dims), 1)
     new_sigma = jnp.sum(jnp.where(row == column, new_sigma_ref[...], 0.0), 1, keepdims=True)
@@ -390,6 +357,30 @@
     new_centers_ref[...] = centers + delta
     new_sigmas_ref[...] = jnp.sqrt((heights * sigmas * sigmas + spread) / new_heights - delta * delta)
 
+    def wait_sends(step, carry):
+        copy_a(peer(step), me).wait_send()
+        copy_b(peer(step), me).wait_send()
+        return carry
+
+    lax.fori_loop(1, kern_count, wait_sends, 0)
+    for step in range(1, walk_count):
+        def wait_send_c(index, carry):
+            copy_c(step, index, my_chunk, walk).wait_send()
+            return carry
+
+        lax.fori_loop(0, chunks, wait_send_c, 0)
+        for copy in copy_w(step, walk):
+            copy.wait_send()
+
+
+def write_kernel(*refs):
+    count = (len(refs) - 1) // 2
+    copies = [pltpu.make_async_copy(refs[i], refs[count + i], refs[-1].at[i]) for i in range(count)]
+    for copy in copies:
+        copy.start()
+    for copy in copies:
+        copy.wait()
+
 
 def per_device(walkers, centers, sigmas, heights, kernel_live, merge_target, new_sigma, norm_old):
     dims, walk_len = walkers.shape
@@ -403,18 +394,11 @@
     height_row = heights.reshape(1, shard_len)
 
     dma = pltpu.SemaphoreType.DMA
-    share, density, packed, packed_slot, packed_density, norm_row = pl.pallas_call(
+    shapes = [(1, walk_len), (dims, walk_len), (1, shard_len), (dims, shard_len), (dims, shard_len), (1, 1)]
+    results = pl.pallas_call(
         functools.partial(sums_kernel, kern_count, walk_count, groups, capacity),
-        out_shape=(
-            jax.ShapeDtypeStruct((kern_count, per + 1, LANES), F32),
-            jax.ShapeDtypeStruct((walk_count, 1, walk_len), F32),
-            jax.ShapeDtypeStruct((walk_count, dims, capacity), F32),
-            jax.ShapeDtypeStruct((walk_count, 1, capacity), F32),
-            jax.ShapeDtypeStruct((walk_count, 1, capacity), F32),
-            jax.ShapeDtypeStruct((1, 1), F32),
-        ),
-        in_specs=[HBM] * 7,
-        out_specs=(VMEM,) * 6,
+        out_shape=[pltpu.VMEM(shape, F32) for shape in shapes],
+        in_specs=[HBM] * 8,
         scratch_shapes=[
             pltpu.VMEM((dims, walk_len), F32),
             pltpu.VMEM((1, walk_len), jnp.int32),
@@ -423,7 +407,8 @@
             pltpu.VMEM((1, shard_len), F32),
             pltpu.SMEM((1,), jnp.int32),
             pltpu.SMEM((1,), F32),
-            dma((7,)),
+            pltpu.VMEM((1, dims), F32),
+            dma((8,)),
             pltpu.VMEM((walk_len // (2 * LANES), LANES, 2 * LANES), BF16),
             pltpu.VMEM((shard_len, LANES), BF16),
             pltpu.VMEM((6 * dims + 16, shard_len), BF16),
@@ -436,30 +421,29 @@
             pltpu.VMEM((walk_count, dims, walk_len), F32),
             pltpu.VMEM((walk_count, 1, walk_len), jnp.int32),
             pltpu.VMEM((walk_count, capacity, walk_len), BF16),
+            pltpu.VMEM((walk_count, shard_len, capacity), BF16),
             dma((kern_count,)), dma((kern_count,)),
             dma((kern_count,)), dma((kern_count,)),
             dma((walk_count, chunks)), dma((walk_count, chunks)),
             dma((walk_count,)), dma((walk_count,)),
             dma((walk_count,)), dma((walk_count,)),
         ],
-        compiler_params=pltpu.CompilerParams(collective_id=0, has_side_effects=True),
+        compiler_params=pltpu.CompilerParams(collective_id=0, has_side_effects=True, vmem_limit_bytes=LIMIT),
         name="sums",
-    )(walkers, merge_target.reshape(1, walk_len), centers, sigmas, height_row, kernel_live, norm_old)
+    )(*[
+        pltpu.with_memory_space_constraint(x, pltpu.HBM)
+        for x in (walkers, merge_target.reshape(1, walk_len), centers, sigmas, height_row)
+    ], kernel_live, norm_old, pltpu.with_memory_space_constraint(new_sigma.reshape(1, dims), pltpu.HBM))
 
     bias, force, new_heights, new_centers, new_sigmas, log_norm = pl.pallas_call(
-        functools.partial(merge_kernel, groups),
-        out_shape=(
-            jax.ShapeDtypeStruct((1, walk_len), F32),
-            jax.ShapeDtypeStruct((dims, walk_len), F32),
-            jax.ShapeDtypeStruct((1, shard_len), F32),
-            jax.ShapeDtypeStruct((dims, shard_len), F32),
-            jax.ShapeDtypeStruct((dims, shard_len), F32),
-            jax.ShapeDtypeStruct((1, 1), F32),
-        ),
-        in_specs=[VMEM] * 10,
-        out_specs=(VMEM,) * 6,
-        name="merge",
-    )(share, density, packed, packed_slot, packed_density, centers, sigmas, height_row, new_sigma.reshape(1, dims), norm_row)
+        write_kernel,
+        out_shape=[jax.ShapeDtypeStruct(shape, F32) for shape in shapes],
+        in_specs=[VMEM] * 6,
+        out_specs=[HBM] * 6,
+        scratch_shapes=[dma((6,))],
+        compiler_params=pltpu.CompilerParams(vmem_limit_bytes=LIMIT),
+        name="write",
+    )(*results)
     return (bias.reshape(walk_len), force, new_heights.reshape(shard_len), new_centers, new_sigmas, log_norm.reshape(1))
 
 

time: 24.3 us -> 23.3 us (0.959)
  Pallas kernels: 22.2 us -> 21.2 us
    pallas_call x1, Pallas kernels: 2.78 us -> 1.36 us  [per_device(): pl.pallas_call(write_kernel, out_shape=[jax.ShapeDtypeStruct(shape, F32)...]
    pallas_call x1, Pallas kernels: 19.4 us -> 19.9 us  [per_device(): pl.pallas_call(functools.partial(sums_kernel, kern_count, walk_count, gro...]
where the time goes in v1:
time: 23.3 us; the launch traced here: 23.1 us
  Pallas kernels  21.2 us (91%)
  between operations  1.93 us (8%)
    pallas_call x1, Pallas kernels, per_device(): pl.pallas_call(functools.partial(sums_kernel, kern_count, walk_count, gro...  19.9 us
    pallas_call x1, Pallas kernels, per_device(): pl.pallas_call(write_kernel, out_shape=[jax.ShapeDtypeStruct(shape, F32)...  1.36 us

profile of v1, /device:TPU:0, one launch (start us, length us, event | category | flops | bytes accessed | tf_op | source)
XLA Modules:
  0.0 23.1 jit_solution(12302791609830789051)
XLA Ops:
  1.9 19.9 %sums.1 = (f32[1,1024]{1,0:T(1,128)S(1)}, f32[8,1024]{1,0:T(8,128)S(1)}, f32[1,2048]{1,0:T(1,128)S(1)}, f32[8,2048]{1,0:T(8,128)S(1)}, f32[8,2048]{1,0:T(8,128)S(1)}, /*index=5*/f32[1,1]{1,0:T(1,128)}) custom-call(f32[8,1024]{1,0:T(8,128)} %walkers_hbm.1, s32[1,1024]{1,0:T(1,128)} %bitcast.7, f32[8,2048]{1,0:T(8,128)} %centers_hbm.1, f32[8,2048]{1,0:T(8,128)} %sigmas_hbm.1, ...), custom_call_target="tpu_custom_call" | custom-call | tf_op jit(solution)/shard_map/sums/pallas_call | solution.py:398
  21.8 1.4 %write.1 = (f32[1,1024]{1,0:T(1,128)}, f32[8,1024]{1,0:T(8,128)}, f32[1,2048]{1,0:T(1,128)}, f32[8,2048]{1,0:T(8,128)}, f32[8,2048]{1,0:T(8,128)}, /*index=5*/f32[1,1]{1,0:T(1,128)}) custom-call(f32[1,1024]{1,0:T(1,128)S(1)} %get-tuple-element.18.refs_0_, f32[8,1024]{1,0:T(8,128)S(1)} %get-tuple-element.19.refs_1_, f32[1,2048]{1,0:T(1,128)S(1)} %get-tuple-element.20.refs_2_, ...), custom_call_target="tpu_custom_call" | custom-call | tf_op jit(solution)/shard_map/write/pallas_call | solution.py:438

commit v2 on v1

v2 whole, which is shorter than its diff:
```python
import functools
import math

import jax
import jax.numpy as jnp
from jax import lax
from jax.experimental import pallas as pl
from jax.experimental.pallas import tpu as pltpu
from jax.sharding import PartitionSpec as P

PREFACTOR = 0.9
EPSILON = 0.01
RATE = 0.25
LANES = 128
LOG2E = math.log2(math.e)
MESH = pl.DeviceIdType.MESH
F32 = jnp.float32
BF16 = jnp.bfloat16
VMEM = pl.BlockSpec(memory_space=pltpu.VMEM)
HBM = pl.BlockSpec(memory_space=pltpu.HBM)
LIMIT = 24 << 20


def split(x):
    high = x.astype(BF16).astype(F32)
    rest = x - high
    middle = rest.astype(BF16).astype(F32)
    low = (rest - middle).astype(BF16).astype(F32)
    return high, middle, low


def row_of(parts, width):
    row = lax.broadcasted_iota(jnp.int32, (8, width), 0)
    block = jnp.zeros((8, width), F32)
    for index, part in enumerate(parts):
        block = jnp.where(row == index, part, block)
    return block


def sums_kernel(kern_count, walk_count, owners, capacity,
                walkers_hbm, target_hbm, centers_hbm, sigmas_hbm, heights_hbm, live_hbm, norm_hbm, new_sigma_hbm,
                bias_ref, force_ref, new_heights_ref, new_centers_ref, new_sigmas_ref,
                walkers_ref, target_ref, centers_ref, sigmas_ref, heights_ref, live_ref, norm_ref, new_sigma_ref, load_sem,
                walker_feat, kernel_feat, kernel_mom, sums, got, early, early_got, early_far, direct, direct_far,
                mine, shared, far, far_walkers, far_targets, table, placing, spare,
                sent, recv_a, recv_d, recv_e, recv_b, recv_w):
    def load(source, target, index):
        return pltpu.make_async_copy(source, target, load_sem.at[index])

    wide = [
        load(walkers_hbm, walkers_ref, 0),
        load(centers_hbm, centers_ref, 0),
        load(sigmas_hbm, sigmas_ref, 0),
        load(heights_hbm, heights_ref, 0),
        load(target_hbm, target_ref, 0),
    ]
    narrow = [load(live_hbm, live_ref, 1), load(norm_hbm, norm_ref, 2), load(new_sigma_hbm, new_sigma_ref, 3)]
    for copy in wide + narrow:
        copy.start()
    dims, walk_len = walkers_ref.shape
    shard_len = centers_ref.shape[1]
    late = kern_count - owners
    rows = dims + 2
    me = lax.axis_index("kern")
    walk = lax.axis_index("walk")
    flat = me * walk_count + walk
    total_count = kern_count * walk_count

    others = walk_count - 1
    load_rows = (dims * (walk_len + 2 * shard_len) + shard_len + walk_len) // LANES
    walker_rows = others * (dims + 1) * walk_len // LANES

    def other(step):
        return lax.rem(walk + step, walk_count)

    def bulk(count, sem):
        view = spare.at[pl.ds(0, count)]
        return pltpu.make_async_remote_copy(
            src_ref=view, dst_ref=view, send_sem=sent, recv_sem=sem, device_id=(me, walk), device_id_type=MESH
        )

    barrier = pltpu.get_barrier_semaphore()

    def greet(step, carry):
        peer = lax.rem(flat + step, total_count)
        pl.semaphore_signal(
            barrier, inc=1, device_id=(peer // walk_count, lax.rem(peer, walk_count)), device_id_type=MESH
        )
        return carry

    lax.fori_loop(1, total_count, greet, 0)

    load(spare.at[pl.ds(0, load_rows)], spare.at[pl.ds(0, load_rows)], 0).wait()
    for copy in narrow:
        copy.wait()
    norm = norm_ref[0]
    walkers = walkers_ref[...]
    sq_h, sq_m, sq_l = split(walkers * walkers)
    wk_h, wk_m, wk_l = split(walkers)
    h, m, l = [sq_h, wk_h], [sq_m, wk_m], [sq_l, wk_l]
    one = jnp.ones((1, walk_len), F32)
    pad = jnp.zeros((LANES - 12 * dims - 8, walk_len), F32)
    stacked = jnp.concatenate(h + m + h + m + l + h + [row_of([one] * 3, walk_len), pad], 0)
    stacked = stacked.astype(BF16)
    width = 2 * LANES
    quarters = walk_len // width
    for quarter in range(quarters):
        walker_feat[quarter] = stacked[:, quarter * width : (quarter + 1) * width]

    centers = centers_ref[...]
    sigmas = sigmas_ref[...]
    inverse_var = 1.0 / (sigmas * sigmas)
    scaled = centers * inverse_var
    constant = jnp.log(heights_ref[...]) - 0.5 * jnp.sum(centers * scaled, 0, keepdims=True)
    k_sq = split((-0.5 * LOG2E) * inverse_var)
    k_lin = split(LOG2E * scaled)
    con = row_of(split(LOG2E * constant), shard_len)
    h, m, l = [[k_sq[i], k_lin[i]] for i in range(3)]
    pad = jnp.zeros((LANES - 12 * dims - 8, shard_len), F32)
    kernel_feat[...] = jnp.concatenate(h + h + m + m + h + l + [con, pad], 0).T.astype(BF16)

    live = live_ref[0]
    alive = (lax.broadcasted_iota(jnp.int32, (8, shard_len), 1) < live).astype(F32)
    mom_a = split(inverse_var * alive)
    mom_c = split(scaled * alive)
    pad = jnp.zeros((8, shard_len), F32)
    mom_rows = [mom_a[0], mom_c[0], mom_a[1], mom_c[1], mom_a[2], mom_c[2], row_of([alive], shard_len), pad]
    kernel_mom[...] = jnp.concatenate(mom_rows, 0).astype(BF16)

    live_row = jnp.full((1, LANES), live, jnp.int32).astype(F32)
    block = min(512, shard_len)

    def copy_a(owner, source):
        return pltpu.make_async_remote_copy(
            src_ref=sums.at[owner], dst_ref=got.at[source],
            send_sem=sent, recv_sem=recv_a.at[jnp.where(me < owners, 0, 1)],
            device_id=(owner, walk), device_id_type=MESH,
        )

    def copy_d(quarter, source):
        part = pl.ds(quarter * 2, 2)
        return pltpu.make_async_remote_copy(
            src_ref=sums.at[part], dst_ref=direct.at[source, part],
            send_sem=sent, recv_sem=recv_d.at[min(quarter, 1)],
            device_id=(0, walk), device_id_type=MESH,
        )

    def copy_g(step, quarter, source, origin):
        part = pl.ds(quarter * 2, 2)
        return pltpu.make_async_remote_copy(
            src_ref=sums.at[part, pl.ds(dims, 1)], dst_ref=direct_far.at[origin, source, part],
            send_sem=sent, recv_sem=recv_d.at[min(quarter, 1)],
            device_id=(0, other(step)), device_id_type=MESH,
        )

    def copy_e(source):
        return pltpu.make_async_remote_copy(
            src_ref=early, dst_ref=early_got.at[source],
            send_sem=sent, recv_sem=recv_e,
            device_id=(0, walk), device_id_type=MESH,
        )

    def copy_h(step, source, origin):
        return pltpu.make_async_remote_copy(
            src_ref=early.at[pl.ds(dims, 1)], dst_ref=early_far.at[origin, source],
            send_sem=sent, recv_sem=recv_e,
            device_id=(0, other(step)), device_id_type=MESH,
        )

    def copy_b(target, source):
        return pltpu.make_async_remote_copy(
            src_ref=mine, dst_ref=shared.at[source],
            send_sem=sent, recv_sem=recv_b,
            device_id=(target, walk), device_id_type=MESH,
        )

    def copy_c(step, target, source, origin):
        return pltpu.make_async_remote_copy(
            src_ref=mine.at[pl.ds(dims, 1)], dst_ref=far.at[origin, source],
            send_sem=sent, recv_sem=recv_b,
            device_id=(target, other(step)), device_id_type=MESH,
        )

    def copy_w(step, source):
        return (
            pltpu.make_async_remote_copy(
                src_ref=walkers_ref, dst_ref=far_walkers.at[source],
                send_sem=sent, recv_sem=recv_w,
                device_id=(me, other(step)), device_id_type=MESH,
            ),
            pltpu.make_async_remote_copy(
                src_ref=target_ref, dst_ref=far_targets.at[source],
                send_sem=sent, recv_sem=recv_w,
                device_id=(me, other(step)), device_id_type=MESH,
            ),
        )

    def compute(quarter):
        feat = walker_feat[quarter]
        moments = None
        for index in range(shard_len // block):
            part = slice(index * block, (index + 1) * block)
            e = jnp.exp2(jnp.dot(kernel_feat[part, :], feat, preferred_element_type=F32))
            high = e.astype(BF16)
            low = (e - high.astype(F32)).astype(BF16)
            moms = kernel_mom[:, part]
            add = jnp.dot(moms, high, preferred_element_type=F32) + jnp.dot(
                moms, low, preferred_element_type=F32
            )
            moments = add if moments is None else moments + add
        a_sum = moments[0:dims] + moments[2 * dims : 3 * dims] + moments[4 * dims : 5 * dims]
        c_sum = moments[dims : 2 * dims] + moments[3 * dims : 4 * dims] + moments[5 * dims : 6 * dims]
        density = moments[6 * dims : 6 * dims + 1]
        grad = c_sum - walkers_ref[:, quarter * width : (quarter + 1) * width] * a_sum
        for chunk in range(2):
            part = slice(chunk * LANES, (chunk + 1) * LANES)
            sums[quarter * 2 + chunk, 0:dims, :] = grad[:, part]
            sums[quarter * 2 + chunk, dims : dims + 1, :] = density[:, part]
            sums[quarter * 2 + chunk, dims + 1 : dims + 2, :] = live_row

    def sends_a(owner):
        return (me != owner) & (me < owners) if owner == 0 else me != owner

    def send(quarter):
        @pl.when(me >= owners)
        def _():
            copy_d(quarter, me - owners).start()
            for step in range(1, walk_count):
                copy_g(step, quarter, me - owners, walk).start()

        for owner in (2 * quarter, 2 * quarter + 1):
            @pl.when(sends_a(owner))
            def _():
                copy_a(owner, me).start()

    for quarter in range(quarters):
        compute(quarter)
        if quarter == 1:
            pl.semaphore_wait(barrier, total_count - 1)
            send(0)
            for step in range(1, walk_count):
                for copy in copy_w(step, walk):
                    copy.start()
        if quarter >= 1:
            send(quarter)

    far_walkers[walk] = walkers
    far_targets[walk] = target_ref[...]
    bulk(walker_rows, recv_w).wait_recv()
    targets = [far_targets[index] for index in range(walk_count)]
    if walk_count % 8:
        targets.append(jnp.full((8 - walk_count % 8, walk_len), -1, jnp.int32))
    local = jnp.concatenate(targets, 0) - me * shard_len
    owned = (local >= 0) & (local < shard_len)
    before = lax.broadcasted_iota(jnp.int32, (walk_len, walk_len), 0) < lax.broadcasted_iota(
        jnp.int32, (walk_len, walk_len), 1
    )
    place = jnp.dot(
        jnp.where(owned, 1.0, 0.0).astype(BF16),
        jnp.where(before, 1.0, 0.0).astype(BF16),
        preferred_element_type=F32,
    )
    place = jnp.where(owned, place, -1.0)
    slot = jnp.where(owned, (local + 1).astype(F32), 0.0)
    want = lax.broadcasted_iota(jnp.int32, (capacity, walk_len), 0).astype(F32)

    def pack(feat, index):
        return lax.dot_general(
            feat.astype(BF16), table[index], (((1,), (1,)), ((), ())), preferred_element_type=F32
        )

    slots = lax.broadcasted_iota(jnp.int32, (shard_len, capacity), 0).astype(F32)
    packed_walkers = []
    for index in range(walk_count):
        table[index] = jnp.where(want == place[index : index + 1], 1.0, 0.0).astype(BF16)
        high, middle, low = split(far_walkers[index])
        slot_rows = row_of(split(slot[index : index + 1]), walk_len)
        packed = pack(jnp.concatenate([high, middle, low, slot_rows], 0), index)
        packed_walkers.append(packed[0:dims] + (packed[dims : 2 * dims] + packed[2 * dims : 3 * dims]))
        at = 3 * dims
        packed_slot = packed[at : at + 1] + packed[at + 1 : at + 2] + packed[at + 2 : at + 3] - 1.0
        placing[index] = jnp.where(slots == packed_slot, 1.0, 0.0).astype(BF16)

    def finish(total):
        live_total = total[dims + 1 : dims + 2]
        density = total[dims : dims + 1] / live_total
        ratio = density / norm + EPSILON
        return density, -PREFACTOR * (total[0:dims] / live_total) / (norm * ratio)

    def publish(total):
        density, force = finish(total)
        mine[0:dims, :] = force
        mine[dims : dims + 1, :] = density

        def start_b(target, carry):
            @pl.when(target != me)
            def _():
                copy_b(target, me).start()

            for step in range(1, walk_count):
                copy_c(step, target, me, walk).start()
            return carry

        lax.fori_loop(1, kern_count, start_b, 0)
        shared[me, 0:dims, :] = force
        shared[me, dims : dims + 1, :] = density

    @pl.when(me < owners)
    def _():
        got[me] = sums[me]

        bulk((owners - 1) * rows, recv_a.at[0]).wait_recv()
        total = got[0]
        for source in range(1, owners):
            total = total + got[source]
        early[...] = total
        for step in range(1, walk_count):
            copy_h(step, me, walk).start()

        @pl.when(me > 0)
        def _():
            copy_e(me).start()

            bulk(late * rows, recv_a.at[1]).wait_recv()
            whole = total
            for source in range(owners, kern_count):
                whole = whole + got[source]
            publish(whole)

        @pl.when(me == 0)
        def _():
            def late_sum(chunk, whole):
                for source in range(late):
                    whole = whole + direct[source, chunk]
                return whole

            bulk(late * 2 * (rows + others), recv_d.at[0]).wait_recv()
            publish(late_sum(0, total))

            bulk((owners - 1) * rows + others * owners, recv_e).wait_recv()
            bulk(late * (owners - 2) * (rows + others), recv_d.at[1]).wait_recv()
            for chunk in range(1, owners):
                density, force = finish(late_sum(chunk, early_got[chunk]))
                shared[chunk, 0:dims, :] = force
                shared[chunk, dims : dims + 1, :] = density
            live_total = late_sum(0, total)[dims + 1 : dims + 2]
            for step in range(1, walk_count):
                origin = other(step)
                for chunk in range(owners):
                    whole = early_far[origin, chunk]
                    for source in range(late):
                        whole = whole + direct_far[origin, source, chunk]
                    far[origin, chunk] = whole / live_total

    @pl.when((me > 0) & (me < owners))
    def _():
        bulk((owners - 1) * (dims + 1) + others * owners, recv_b).wait_recv()

    @pl.when(me >= owners)
    def _():
        bulk(owners * (dims + 1) + others * owners, recv_b).wait_recv()

    def biased(density):
        return PREFACTOR * jnp.log(density / norm + EPSILON)

    for chunk in range(owners):
        part = slice(chunk * LANES, (chunk + 1) * LANES)
        density = shared[chunk, dims : dims + 1, :]
        far[walk, chunk] = density
        bias_ref[:, part] = biased(density)
        force_ref[:, part] = shared[chunk, 0:dims, :]
    density_sum = jnp.zeros((1, 1), F32)
    merged = None
    for index in range(walk_count):
        whole = jnp.concatenate([far[index, chunk] for chunk in range(owners)], 1)
        density_sum = density_sum + jnp.sum(whole, 1, keepdims=True)
        packed = pack(row_of(split(whole), walk_len), index)
        weight = jnp.exp(biased(packed[0:1] + packed[1:2] + packed[2:3]))
        lin = split(weight * packed_walkers[index])
        sq = split(weight * (packed_walkers[index] * packed_walkers[index]))
        last = row_of(split(weight), capacity)
        pad = jnp.zeros((8, capacity), F32)
        feat = jnp.concatenate([lin[0], sq[0], lin[1], sq[1], lin[2], sq[2], last, pad], 0).astype(BF16)
        add = lax.dot_general(feat, placing[index], (((1,), (1,)), ((), ())), preferred_element_type=F32)
        merged = add if merged is None else merged + add
    log_norm = jnp.log((1.0 - RATE) * norm + RATE * density_sum / (walk_len * walk_count))
    bias_ref[:, walk_len : walk_len + LANES] = jnp.broadcast_to(log_norm, (1, LANES))

    first = merged[0:dims] + (merged[2 * dims : 3 * dims] + merged[4 * dims : 5 * dims])
    second = merged[dims : 2 * dims] + (merged[3 * dims : 4 * dims] + merged[5 * dims : 6 * dims])
    at = 6 * dims
    gain = merged[at : at + 1] + (merged[at + 1 : at + 2] + merged[at + 2 : at + 3])
    row = lax.broadcasted_iota(jnp.int32, (dims, dims), 0)
    column = lax.broadcasted_iota(jnp.int32, (dims, dims), 1)
    new_sigma = jnp.sum(jnp.where(row == column, new_sigma_ref[...], 0.0), 1, keepdims=True)
    centers = centers_ref[...]
    sigmas = sigmas_ref[...]
    heights = heights_ref[...]
    shift = first - centers * gain
    spread = second - 2.0 * centers * first + centers * centers * gain + new_sigma * new_sigma * gain
    new_heights = heights + gain
    delta = shift / new_heights
    new_heights_ref[...] = new_heights
    new_centers_ref[...] = centers + delta
    new_sigmas_ref[...] = jnp.sqrt((heights * sigmas * sigmas + spread) / new_heights - delta * delta)

    always = walker_rows + (owners - 1) * rows
    answers = others * (kern_count - 1) + (kern_count - 2) * (dims + 1) + others

    @pl.when(me >= owners)
    def _():
        bulk(always + owners * (rows + others), sent).wait_send()

    @pl.when((me > 0) & (me < owners))
    def _():
        bulk(always + answers + rows, sent).wait_send()

    @pl.when(me == 0)
    def _():
        bulk(always + answers + dims + 1, sent).wait_send()


def write_kernel(bias_ref, force_ref, new_heights_ref, new_centers_ref, new_sigmas_ref,
                 bias_hbm, force_hbm, new_heights_hbm, new_centers_hbm, new_sigmas_hbm, log_norm_hbm, log_norm_ref, sem):
    walk_len = bias_hbm.shape[1]
    log_norm_ref[...] = bias_ref[:, walk_len : walk_len + 1]
    pairs = [
        (new_centers_ref, new_centers_hbm),
        (new_sigmas_ref, new_sigmas_hbm),
        (force_ref, force_hbm),
        (new_heights_ref, new_heights_hbm),
        (bias_ref.at[:, pl.ds(0, walk_len)], bias_hbm),
        (log_norm_ref, log_norm_hbm),
    ]
    copies = [pltpu.make_async_copy(source, target, sem.at[index]) for index, (source, target) in enumerate(pairs)]
    for copy in copies:
        copy.start()
    for copy in copies:
        copy.wait()


def per_device(walkers, centers, sigmas, heights, kernel_live, merge_target, new_sigma, norm_old):
    dims, walk_len = walkers.shape
    shard_len = centers.shape[1]
    kern_count = lax.axis_size("kern")
    walk_count = lax.axis_size("walk")
    owners = walk_len // LANES
    late = kern_count - owners
    quarters = owners // 2
    rows = dims + 2
    capacity = 2 * walk_len // kern_count
    height_row = heights.reshape(1, shard_len)
    load_rows = (dims * (walk_len + 2 * shard_len) + shard_len + walk_len) // LANES
    walker_rows = walk_count * (dims + 1) * walk_len // LANES
    answer_rows = walk_count * kern_count + kern_count * rows
    spare_rows = load_rows + walker_rows + answer_rows + kern_count * owners * (rows + walk_count)

    dma = pltpu.SemaphoreType.DMA
    shapes = [(1, walk_len), (dims, walk_len), (1, shard_len), (dims, shard_len), (dims, shard_len), (1, 1)]
    results = pl.pallas_call(
        functools.partial(sums_kernel, kern_count, walk_count, owners, capacity),
        out_shape=[pltpu.VMEM(shape, F32) for shape in [(1, walk_len + LANES)] + shapes[1:5]],
        in_specs=[HBM] * 8,
        scratch_shapes=[
            pltpu.VMEM((dims, walk_len), F32),
            pltpu.VMEM((1, walk_len), jnp.int32),
            pltpu.VMEM((dims, shard_len), F32),
            pltpu.VMEM((dims, shard_len), F32),
            pltpu.VMEM((1, shard_len), F32),
            pltpu.SMEM((1,), jnp.int32),
            pltpu.SMEM((1,), F32),
            pltpu.VMEM((1, dims), F32),
            dma((4,)),
            pltpu.VMEM((walk_len // (2 * LANES), LANES, 2 * LANES), BF16),
            pltpu.VMEM((shard_len, LANES), BF16),
            pltpu.VMEM((6 * dims + 16, shard_len), BF16),
            pltpu.VMEM((owners, rows, LANES), F32),
            pltpu.VMEM((kern_count, rows, LANES), F32),
            pltpu.VMEM((rows, LANES), F32),
            pltpu.VMEM((owners, rows, LANES), F32),
            pltpu.VMEM((walk_count, owners, 1, LANES), F32),
            pltpu.VMEM((late, owners, rows, LANES), F32),
            pltpu.VMEM((walk_count, late, owners, 1, LANES), F32),
            pltpu.VMEM((dims + 1, LANES), F32),
            pltpu.VMEM((owners, dims + 1, LANES), F32),
            pltpu.VMEM((walk_count, owners, 1, LANES), F32),
            pltpu.VMEM((walk_count, dims, walk_len), F32),
            pltpu.VMEM((walk_count, 1, walk_len), jnp.int32),
            pltpu.VMEM((walk_count, capacity, walk_len), BF16),
            pltpu.VMEM((walk_count, shard_len, capacity), BF16),
            pltpu.VMEM((spare_rows, LANES), F32),
            dma, dma((2,)), dma((2,)), dma, dma, dma,
        ],
        compiler_params=pltpu.CompilerParams(collective_id=0, has_side_effects=True, vmem_limit_bytes=LIMIT),
        name="sums",
    )(*[
        pltpu.with_memory_space_constraint(x, pltpu.HBM)
        for x in (walkers, merge_target.reshape(1, walk_len), centers, sigmas, height_row)
    ], kernel_live, norm_old, pltpu.with_memory_space_constraint(new_sigma.reshape(1, dims), pltpu.HBM))

    bias, force, new_heights, new_centers, new_sigmas, log_norm = pl.pallas_call(
        write_kernel,
        out_shape=[jax.ShapeDtypeStruct(shape, F32) for shape in shapes],
        in_specs=[VMEM] * 5,
        out_specs=[HBM] * 6,
        scratch_shapes=[pltpu.VMEM((1, 1), F32), dma((6,))],
        compiler_params=pltpu.CompilerParams(vmem_limit_bytes=LIMIT),
        name="write",
    )(*results)
    return (bias.reshape(walk_len), force, new_heights.reshape(shard_len), new_centers, new_sigmas, log_norm.reshape(1))


def solution(mesh):
    in_specs = (
        P(None, "walk"),
        P(None, "kern"),
        P(None, "kern"),
        P("kern"),
        P("kern"),
        P("walk"),
        P(),
        P(),
    )
    out_specs = (P("walk"), P(None, "walk"), P("kern"), P(None, "kern"), P(None, "kern"), P())
    return jax.shard_map(
        per_device, mesh=mesh, in_specs=in_specs, out_specs=out_specs, check_vma=False
    )
```

time: 23.3 us -> 19.7 us (0.85)
  Pallas kernels: 21.2 us -> 17.5 us
    pallas_call x1, Pallas kernels: 19.9 us -> 16.8 us  [per_device(): pl.pallas_call(functools.partial(sums_kernel, kern_count, walk_count, own...]
    pallas_call x1, Pallas kernels: 1.36 us -> 0.72 us  [per_device(): pl.pallas_call(write_kernel, out_shape=[jax.ShapeDtypeStruct(shape, F32)...]
where the time goes in v2:
time: 19.7 us; the launch traced here: 19.5 us
  Pallas kernels  17.5 us (89%)
  between operations  1.93 us (10%)
    pallas_call x1, Pallas kernels, per_device(): pl.pallas_call(functools.partial(sums_kernel, kern_count, walk_count, own...  16.8 us
    pallas_call x1, Pallas kernels, per_device(): pl.pallas_call(write_kernel, out_shape=[jax.ShapeDtypeStruct(shape, F32)...  0.72 us

profile of v2, /device:TPU:0, one launch (start us, length us, event | category | flops | bytes accessed | tf_op | source)
XLA Modules:
  0.0 19.5 jit_solution(7226309064962381752)
XLA Ops:
  1.9 16.8 %sums.1 = (f32[1,1152]{1,0:T(1,128)S(1)}, f32[8,1024]{1,0:T(8,128)S(1)}, f32[1,2048]{1,0:T(1,128)S(1)}, f32[8,2048]{1,0:T(8,128)S(1)}, f32[8,2048]{1,0:T(8,128)S(1)}) custom-call(f32[8,1024]{1,0:T(8,128)} %walkers_hbm.1, s32[1,1024]{1,0:T(1,128)} %bitcast.7, f32[8,2048]{1,0:T(8,128)} %centers_hbm.1, f32[8,2048]{1,0:T(8,128)} %sigmas_hbm.1, ...), custom_call_target="tpu_custom_call" | custom-call | tf_op jit(solution)/shard_map/sums/pallas_call | solution.py:460
  18.8 0.7 %write.1 = (f32[1,1024]{1,0:T(1,128)}, f32[8,1024]{1,0:T(8,128)}, f32[1,2048]{1,0:T(1,128)}, f32[8,2048]{1,0:T(8,128)}, f32[8,2048]{1,0:T(8,128)}, /*index=5*/f32[1,1]{1,0:T(1,128)}) custom-call(f32[1,1152]{1,0:T(1,128)S(1)} %get-tuple-element.17.bias_ref, f32[8,1024]{1,0:T(8,128)S(1)} %get-tuple-element.18.force_ref, ...), custom_call_target="tpu_custom_call" | custom-call | tf_op jit(solution)/shard_map/write/pallas_call | solution.py:501

commit v3 on v2

--- a/solution.py
+++ b/solution.py
@@ -43,7 +43,7 @@
                 walkers_ref, target_ref, centers_ref, sigmas_ref, heights_ref, live_ref, norm_ref, new_sigma_ref, load_sem,
                 walker_feat, kernel_feat, kernel_mom, sums, got, early, early_got, early_far, direct, direct_far,
                 mine, shared, far, far_walkers, far_targets, table, placing, spare,
-                sent, recv_a, recv_d, recv_e, recv_b, recv_w):
+                ready, sent, recv_a, recv_d, recv_e, recv_b, recv_w):
     def load(source, target, index):
         return pltpu.make_async_copy(source, target, load_sem.at[index])
 
@@ -81,14 +81,23 @@
 
     barrier = pltpu.get_barrier_semaphore()
 
-    def greet(step, carry):
-        peer = lax.rem(flat + step, total_count)
+    def greet(peer):
         pl.semaphore_signal(
             barrier, inc=1, device_id=(peer // walk_count, lax.rem(peer, walk_count)), device_id_type=MESH
         )
-        return carry
-
-    lax.fori_loop(1, total_count, greet, 0)
+
+    @pl.when(me < owners)
+    def _():
+        def greet_all(step, carry):
+            greet(lax.rem(flat + step, total_count))
+            return carry
+
+        lax.fori_loop(1, total_count, greet_all, 0)
+
+    @pl.when(me >= owners)
+    def _():
+        for step in range(1, walk_count):
+            greet(me * walk_count + other(step))
 
     load(spare.at[pl.ds(0, load_rows)], spare.at[pl.ds(0, load_rows)], 0).wait()
     for copy in narrow:
@@ -236,7 +245,22 @@
     for quarter in range(quarters):
         compute(quarter)
         if quarter == 1:
-            pl.semaphore_wait(barrier, total_count - 1)
+            @pl.when(me < owners)
+            def _():
+                pl.semaphore_wait(barrier, owners * walk_count - 1)
+
+            @pl.when(me >= owners)
+            def _():
+                pl.semaphore_wait(barrier, owners * walk_count + others)
+
+                def tell(peer, carry):
+                    pl.semaphore_signal(
+                        ready, inc=1, device_id=(peer // walk_count, lax.rem(peer, walk_count)), device_id_type=MESH
+                    )
+                    return carry
+
+                lax.fori_loop(0, owners * walk_count, tell, 0)
+
             send(0)
             for step in range(1, walk_count):
                 for copy in copy_w(step, walk):
@@ -288,6 +312,7 @@
         return density, -PREFACTOR * (total[0:dims] / live_total) / (norm * ratio)
 
     def publish(total):
+        pl.semaphore_wait(ready, late * walk_count)
         density, force = finish(total)
         mine[0:dims, :] = force
         mine[dims : dims + 1, :] = density
@@ -489,7 +514,7 @@
             pltpu.VMEM((walk_count, capacity, walk_len), BF16),
             pltpu.VMEM((walk_count, shard_len, capacity), BF16),
             pltpu.VMEM((spare_rows, LANES), F32),
-            dma, dma((2,)), dma((2,)), dma, dma, dma,
+            pltpu.SemaphoreType.REGULAR, dma, dma((2,)), dma((2,)), dma, dma, dma,
         ],
         compiler_params=pltpu.CompilerParams(collective_id=0, has_side_effects=True, vmem_limit_bytes=LIMIT),
         name="sums",

time: 19.7 us -> 17.9 us (0.909)
  Pallas kernels: 17.5 us -> 15.8 us
    pallas_call x1, Pallas kernels: 16.8 us -> 15.1 us  [per_device(): pl.pallas_call(functools.partial(sums_kernel, kern_count, walk_count, own...]
where the time goes in v3:
time: 17.9 us; the launch traced here: 17.8 us
  Pallas kernels  15.8 us (88%)
  between operations  1.93 us (11%)
    pallas_call x1, Pallas kernels, per_device(): pl.pallas_call(functools.partial(sums_kernel, kern_count, walk_count, own...  15.1 us
    pallas_call x1, Pallas kernels, per_device(): pl.pallas_call(write_kernel, out_shape=[jax.ShapeDtypeStruct(shape, F32)...  0.72 us

profile of v3, /device:TPU:0, one launch (start us, length us, event | category | flops | bytes accessed | tf_op | source)
XLA Modules:
  0.0 17.8 jit_solution(11145323687033671429)
XLA Ops:
  1.9 15.1 %sums.1 = (f32[1,1152]{1,0:T(1,128)S(1)}, f32[8,1024]{1,0:T(8,128)S(1)}, f32[1,2048]{1,0:T(1,128)S(1)}, f32[8,2048]{1,0:T(8,128)S(1)}, f32[8,2048]{1,0:T(8,128)S(1)}) custom-call(f32[8,1024]{1,0:T(8,128)} %walkers_hbm.1, s32[1,1024]{1,0:T(1,128)} %bitcast.7, f32[8,2048]{1,0:T(8,128)} %centers_hbm.1, f32[8,2048]{1,0:T(8,128)} %sigmas_hbm.1, ...), custom_call_target="tpu_custom_call" | custom-call | tf_op jit(solution)/shard_map/sums/pallas_call | solution.py:485
  17.0 0.7 %write.1 = (f32[1,1024]{1,0:T(1,128)}, f32[8,1024]{1,0:T(8,128)}, f32[1,2048]{1,0:T(1,128)}, f32[8,2048]{1,0:T(8,128)}, f32[8,2048]{1,0:T(8,128)}, /*index=5*/f32[1,1]{1,0:T(1,128)}) custom-call(f32[1,1152]{1,0:T(1,128)S(1)} %get-tuple-element.17.bias_ref, f32[8,1024]{1,0:T(8,128)S(1)} %get-tuple-element.18.force_ref, ...), custom_call_target="tpu_custom_call" | custom-call | tf_op jit(solution)/shard_map/write/pallas_call | solution.py:526

commit v4 on v3

--- a/solution.py
+++ b/solution.py
@@ -15,6 +15,7 @@
 LOG2E = math.log2(math.e)
 MESH = pl.DeviceIdType.MESH
 F32 = jnp.float32
+DIRECT = 2
 BF16 = jnp.bfloat16
 VMEM = pl.BlockSpec(memory_space=pltpu.VMEM)
 HBM = pl.BlockSpec(memory_space=pltpu.HBM)
@@ -43,7 +44,7 @@
                 walkers_ref, target_ref, centers_ref, sigmas_ref, heights_ref, live_ref, norm_ref, new_sigma_ref, load_sem,
                 walker_feat, kernel_feat, kernel_mom, sums, got, early, early_got, early_far, direct, direct_far,
                 mine, shared, far, far_walkers, far_targets, table, placing, spare,
-                ready, sent, recv_a, recv_d, recv_e, recv_b, recv_w):
+                sent, recv_a, recv_d, recv_e, recv_b, recv_w):
     def load(source, target, index):
         return pltpu.make_async_copy(source, target, load_sem.at[index])
 
@@ -61,6 +62,8 @@
     shard_len = centers_ref.shape[1]
     late = kern_count - owners
     rows = dims + 2
+    tail = owners - 2 * DIRECT
+    tails = owners - tail
     me = lax.axis_index("kern")
     walk = lax.axis_index("walk")
     flat = me * walk_count + walk
@@ -142,36 +145,34 @@
     def copy_a(owner, source):
         return pltpu.make_async_remote_copy(
             src_ref=sums.at[owner], dst_ref=got.at[source],
-            send_sem=sent, recv_sem=recv_a.at[jnp.where(me < owners, 0, 1)],
+            send_sem=sent, recv_sem=recv_a.at[0 if owner < tail else jnp.where((me > 0) & (me < owners), 0, 1)],
             device_id=(owner, walk), device_id_type=MESH,
         )
 
-    def copy_d(quarter, source):
-        part = pl.ds(quarter * 2, 2)
-        return pltpu.make_async_remote_copy(
-            src_ref=sums.at[part], dst_ref=direct.at[source, part],
-            send_sem=sent, recv_sem=recv_d.at[min(quarter, 1)],
+    def copy_d(chunk):
+        return pltpu.make_async_remote_copy(
+            src_ref=sums.at[pl.ds(chunk, 2)], dst_ref=direct.at[me - owners, pl.ds(chunk - tail, 2)],
+            send_sem=sent, recv_sem=recv_d,
             device_id=(0, walk), device_id_type=MESH,
         )
 
-    def copy_g(step, quarter, source, origin):
-        part = pl.ds(quarter * 2, 2)
-        return pltpu.make_async_remote_copy(
-            src_ref=sums.at[part, pl.ds(dims, 1)], dst_ref=direct_far.at[origin, source, part],
-            send_sem=sent, recv_sem=recv_d.at[min(quarter, 1)],
+    def copy_g(step, slot, chunk):
+        return pltpu.make_async_remote_copy(
+            src_ref=sums.at[pl.ds(chunk, 2), pl.ds(dims, 1)], dst_ref=direct_far.at[walk, slot, pl.ds(chunk - tail, 2)],
+            send_sem=sent, recv_sem=recv_d,
             device_id=(0, other(step)), device_id_type=MESH,
         )
 
-    def copy_e(source):
-        return pltpu.make_async_remote_copy(
-            src_ref=early, dst_ref=early_got.at[source],
+    def copy_e():
+        return pltpu.make_async_remote_copy(
+            src_ref=early, dst_ref=early_got.at[me - tail],
             send_sem=sent, recv_sem=recv_e,
             device_id=(0, walk), device_id_type=MESH,
         )
 
-    def copy_h(step, source, origin):
-        return pltpu.make_async_remote_copy(
-            src_ref=early.at[pl.ds(dims, 1)], dst_ref=early_far.at[origin, source],
+    def copy_h(step):
+        return pltpu.make_async_remote_copy(
+            src_ref=early.at[pl.ds(dims, 1)], dst_ref=early_far.at[walk, me - tail],
             send_sem=sent, recv_sem=recv_e,
             device_id=(0, other(step)), device_id_type=MESH,
         )
@@ -228,45 +229,49 @@
             sums[quarter * 2 + chunk, dims + 1 : dims + 2, :] = live_row
 
     def sends_a(owner):
-        return (me != owner) & (me < owners) if owner == 0 else me != owner
+        return me != owner
 
     def send(quarter):
-        @pl.when(me >= owners)
-        def _():
-            copy_d(quarter, me - owners).start()
-            for step in range(1, walk_count):
-                copy_g(step, quarter, me - owners, walk).start()
+        if 2 * quarter >= tail:
+            @pl.when(me >= owners)
+            def _():
+                copy_d(2 * quarter).start()
+                for step in range(1, walk_count):
+                    copy_g(step, me - owners, 2 * quarter).start()
+
+            @pl.when(me == 0)
+            def _():
+                for step in range(1, walk_count):
+                    copy_g(step, late, 2 * quarter).start()
 
         for owner in (2 * quarter, 2 * quarter + 1):
             @pl.when(sends_a(owner))
             def _():
                 copy_a(owner, me).start()
 
-    for quarter in range(quarters):
-        compute(quarter)
-        if quarter == 1:
-            @pl.when(me < owners)
-            def _():
-                pl.semaphore_wait(barrier, owners * walk_count - 1)
-
-            @pl.when(me >= owners)
-            def _():
+    begin = 0
+    for end in (quarters // 2, quarters):
+        for quarter in range(begin, end):
+            compute(quarter)
+
+        @pl.when(me >= owners)
+        def _():
+            if begin == 0:
                 pl.semaphore_wait(barrier, owners * walk_count + others)
-
-                def tell(peer, carry):
-                    pl.semaphore_signal(
-                        ready, inc=1, device_id=(peer // walk_count, lax.rem(peer, walk_count)), device_id_type=MESH
-                    )
-                    return carry
-
-                lax.fori_loop(0, owners * walk_count, tell, 0)
-
-            send(0)
-            for step in range(1, walk_count):
-                for copy in copy_w(step, walk):
-                    copy.start()
-        if quarter >= 1:
+            for quarter in range(begin, end):
+                send(quarter)
+
+        begin = end
+
+    @pl.when(me < owners)
+    def _():
+        pl.semaphore_wait(barrier, owners * walk_count - 1)
+        for quarter in range(quarters):
             send(quarter)
+
+    for step in range(1, walk_count):
+        for copy in copy_w(step, walk):
+            copy.start()
 
     far_walkers[walk] = walkers
     far_targets[walk] = target_ref[...]
@@ -311,8 +316,7 @@
         ratio = density / norm + EPSILON
         return density, -PREFACTOR * (total[0:dims] / live_total) / (norm * ratio)
 
-    def publish(total):
-        pl.semaphore_wait(ready, late * walk_count)
+    def publish(total, begin):
         density, force = finish(total)
         mine[0:dims, :] = force
         mine[dims : dims + 1, :] = density
@@ -326,56 +330,54 @@
                 copy_c(step, target, me, walk).start()
             return carry
 
-        lax.fori_loop(1, kern_count, start_b, 0)
+        lax.fori_loop(begin, kern_count, start_b, 0)
         shared[me, 0:dims, :] = force
         shared[me, dims : dims + 1, :] = density
 
-    @pl.when(me < owners)
+    @pl.when(me < tail)
     def _():
         got[me] = sums[me]
-
-        bulk((owners - 1) * rows, recv_a.at[0]).wait_recv()
+        bulk((kern_count - 1) * rows, recv_a.at[0]).wait_recv()
         total = got[0]
-        for source in range(1, owners):
+        for source in range(1, kern_count):
+            total = total + got[source]
+        publish(total, 0)
+
+    @pl.when((me >= tail) & (me < owners))
+    def _():
+        got[me] = sums[me]
+        bulk((owners - 2) * rows, recv_a.at[0]).wait_recv()
+        total = got[1]
+        for source in range(2, owners):
             total = total + got[source]
         early[...] = total
+        copy_e().start()
         for step in range(1, walk_count):
-            copy_h(step, me, walk).start()
-
-        @pl.when(me > 0)
-        def _():
-            copy_e(me).start()
-
-            bulk(late * rows, recv_a.at[1]).wait_recv()
-            whole = total
-            for source in range(owners, kern_count):
-                whole = whole + got[source]
-            publish(whole)
-
-        @pl.when(me == 0)
-        def _():
-            def late_sum(chunk, whole):
-                for source in range(late):
-                    whole = whole + direct[source, chunk]
-                return whole
-
-            bulk(late * 2 * (rows + others), recv_d.at[0]).wait_recv()
-            publish(late_sum(0, total))
-
-            bulk((owners - 1) * rows + others * owners, recv_e).wait_recv()
-            bulk(late * (owners - 2) * (rows + others), recv_d.at[1]).wait_recv()
-            for chunk in range(1, owners):
-                density, force = finish(late_sum(chunk, early_got[chunk]))
-                shared[chunk, 0:dims, :] = force
-                shared[chunk, dims : dims + 1, :] = density
-            live_total = late_sum(0, total)[dims + 1 : dims + 2]
+            copy_h(step).start()
+        bulk((late + 1) * rows, recv_a.at[1]).wait_recv()
+        whole = total + got[0]
+        for source in range(owners, kern_count):
+            whole = whole + got[source]
+        publish(whole, 1)
+
+    @pl.when(me == 0)
+    def _():
+        bulk((tail - 1) * (dims + 1) + others * tail, recv_b).wait_recv()
+        bulk(tails * (rows + others), recv_e).wait_recv()
+        bulk(tails * (late * (rows + others) + others), recv_d).wait_recv()
+        for index in range(tails):
+            whole = early_got[index] + sums[tail + index]
+            for source in range(late):
+                whole = whole + direct[source, index]
+            density, force = finish(whole)
+            shared[tail + index, 0:dims, :] = force
+            shared[tail + index, dims : dims + 1, :] = density
             for step in range(1, walk_count):
                 origin = other(step)
-                for chunk in range(owners):
-                    whole = early_far[origin, chunk]
-                    for source in range(late):
-                        whole = whole + direct_far[origin, source, chunk]
-                    far[origin, chunk] = whole / live_total
+                distant = early_far[origin, index]
+                for source in range(late + 1):
+                    distant = distant + direct_far[origin, source, index]
+                far[origin, tail + index] = distant / whole[dims + 1 : dims + 2]
 
     @pl.when((me > 0) & (me < owners))
     def _():
@@ -430,19 +432,22 @@
     new_sigmas_ref[...] = jnp.sqrt((heights * sigmas * sigmas + spread) / new_heights - delta * delta)
 
     always = walker_rows + (owners - 1) * rows
-    answers = others * (kern_count - 1) + (kern_count - 2) * (dims + 1) + others
 
     @pl.when(me >= owners)
     def _():
-        bulk(always + owners * (rows + others), sent).wait_send()
-
-    @pl.when((me > 0) & (me < owners))
-    def _():
-        bulk(always + answers + rows, sent).wait_send()
+        bulk(always + rows + tails * (rows + others), sent).wait_send()
+
+    @pl.when((me > 0) & (me < tail))
+    def _():
+        bulk(always + (kern_count - 1) * (dims + 1) + others * kern_count, sent).wait_send()
 
     @pl.when(me == 0)
     def _():
-        bulk(always + answers + dims + 1, sent).wait_send()
+        bulk(always + (kern_count - 1) * (dims + 1) + others * (kern_count + tails), sent).wait_send()
+
+    @pl.when((me >= tail) & (me < owners))
+    def _():
+        bulk(always + rows + (kern_count - 2) * (dims + 1) + others * kern_count, sent).wait_send()
 
 
 def write_kernel(bias_ref, force_ref, new_heights_ref, new_centers_ref, new_sigmas_ref,
@@ -502,10 +507,10 @@
             pltpu.VMEM((owners, rows, LANES), F32),
             pltpu.VMEM((kern_count, rows, LANES), F32),
             pltpu.VMEM((rows, LANES), F32),
-            pltpu.VMEM((owners, rows, LANES), F32),
-            pltpu.VMEM((walk_count, owners, 1, LANES), F32),
-            pltpu.VMEM((late, owners, rows, LANES), F32),
-            pltpu.VMEM((walk_count, late, owners, 1, LANES), F32),
+            pltpu.VMEM((2 * DIRECT, rows, LANES), F32),
+            pltpu.VMEM((walk_count, 2 * DIRECT, 1, LANES), F32),
+            pltpu.VMEM((late, 2 * DIRECT, rows, LANES), F32),
+            pltpu.VMEM((walk_count, late + 1, 2 * DIRECT, 1, LANES), F32),
             pltpu.VMEM((dims + 1, LANES), F32),
             pltpu.VMEM((owners, dims + 1, LANES), F32),
             pltpu.VMEM((walk_count, owners, 1, LANES), F32),
@@ -514,7 +519,7 @@
             pltpu.VMEM((walk_count, capacity, walk_len), BF16),
             pltpu.VMEM((walk_count, shard_len, capacity), BF16),
             pltpu.VMEM((spare_rows, LANES), F32),
-            pltpu.SemaphoreType.REGULAR, dma, dma((2,)), dma((2,)), dma, dma, dma,
+            dma, dma((2,)), dma, dma, dma, dma,
         ],
         compiler_params=pltpu.CompilerParams(collective_id=0, has_side_effects=True, vmem_limit_bytes=LIMIT),
         name="sums",

time: 17.9 us -> 17.5 us (0.978)
  the two profiles are of different devices: /device:TPU:0 before, /device:TPU:3 now
where the time goes in v4:
time: 17.5 us; the launch traced here: 17.3 us
  Pallas kernels  15.4 us (88%)
  between operations  1.93 us (11%)
    pallas_call x1, Pallas kernels, per_device(): pl.pallas_call(functools.partial(sums_kernel, kern_count, walk_count, own...  14.6 us
    pallas_call x1, Pallas kernels, per_device(): pl.pallas_call(write_kernel, out_shape=[jax.ShapeDtypeStruct(shape, F32)...  0.72 us

profile of v4, /device:TPU:3, one launch (start us, length us, event | category | flops | bytes accessed | tf_op | source)
XLA Modules:
  0.0 17.3 jit_solution(10979921114439717474)
XLA Ops:
  1.9 14.6 %sums.1 = (f32[1,1152]{1,0:T(1,128)S(1)}, f32[8,1024]{1,0:T(8,128)S(1)}, f32[1,2048]{1,0:T(1,128)S(1)}, f32[8,2048]{1,0:T(8,128)S(1)}, f32[8,2048]{1,0:T(8,128)S(1)}) custom-call(f32[8,1024]{1,0:T(8,128)} %walkers_hbm.1, s32[1,1024]{1,0:T(1,128)} %bitcast.7, f32[8,2048]{1,0:T(8,128)} %centers_hbm.1, f32[8,2048]{1,0:T(8,128)} %sigmas_hbm.1, ...), custom_call_target="tpu_custom_call" | custom-call | tf_op jit(solution)/shard_map/sums/pallas_call | solution.py:490
  16.6 0.7 %write.1 = (f32[1,1024]{1,0:T(1,128)}, f32[8,1024]{1,0:T(8,128)}, f32[1,2048]{1,0:T(1,128)}, f32[8,2048]{1,0:T(8,128)}, f32[8,2048]{1,0:T(8,128)}, /*index=5*/f32[1,1]{1,0:T(1,128)}) custom-call(f32[1,1152]{1,0:T(1,128)S(1)} %get-tuple-element.17.bias_ref, f32[8,1024]{1,0:T(8,128)S(1)} %get-tuple-element.18.force_ref, ...), custom_call_target="tpu_custom_call" | custom-call | tf_op jit(solution)/shard_map/write/pallas_call | solution.py:531

commit v5 on v4

--- a/solution.py
+++ b/solution.py
@@ -289,26 +289,45 @@
         jnp.where(before, 1.0, 0.0).astype(BF16),
         preferred_element_type=F32,
     )
-    place = jnp.where(owned, place, -1.0)
     slot = jnp.where(owned, (local + 1).astype(F32), 0.0)
-    want = lax.broadcasted_iota(jnp.int32, (capacity, walk_len), 0).astype(F32)
-
-    def pack(feat, index):
-        return lax.dot_general(
-            feat.astype(BF16), table[index], (((1,), (1,)), ((), ())), preferred_element_type=F32
-        )
-
-    slots = lax.broadcasted_iota(jnp.int32, (shard_len, capacity), 0).astype(F32)
-    packed_walkers = []
+
+    def pack(feat):
+        return jnp.dot(feat.astype(BF16), table[...], preferred_element_type=F32)
+
+    def of_walk(index, height):
+        column = lax.broadcasted_iota(jnp.int32, (height, span), 1)
+        return (column >= index * capacity) & (column < (index + 1) * capacity)
+
+    span = walk_count * capacity
+    lane = lax.broadcasted_iota(jnp.int32, (walk_len, LANES), 1).astype(F32)
+    spots = [
+        jnp.broadcast_to(jnp.where(owned[index : index + 1], place[index : index + 1] + index * capacity, -1.0), (LANES, walk_len)).T
+        for index in range(walk_count)
+    ]
+    for at in range(0, span, LANES):
+        hit = lane + at == spots[0]
+        for spot in spots[1:]:
+            hit = hit | (lane + at == spot)
+        table[:, at : at + LANES] = jnp.where(hit, 1.0, 0.0).astype(BF16)
+    packed = jnp.zeros((3 * dims + 8, span), F32)
     for index in range(walk_count):
-        table[index] = jnp.where(want == place[index : index + 1], 1.0, 0.0).astype(BF16)
         high, middle, low = split(far_walkers[index])
         slot_rows = row_of(split(slot[index : index + 1]), walk_len)
-        packed = pack(jnp.concatenate([high, middle, low, slot_rows], 0), index)
-        packed_walkers.append(packed[0:dims] + (packed[dims : 2 * dims] + packed[2 * dims : 3 * dims]))
-        at = 3 * dims
-        packed_slot = packed[at : at + 1] + packed[at + 1 : at + 2] + packed[at + 2 : at + 3] - 1.0
-        placing[index] = jnp.where(slots == packed_slot, 1.0, 0.0).astype(BF16)
+        found = pack(jnp.concatenate([high, middle, low, slot_rows], 0))
+        packed = jnp.where(of_walk(index, 3 * dims + 8), found, packed)
+    packed_walkers = packed[0:dims] + (packed[dims : 2 * dims] + packed[2 * dims : 3 * dims])
+    at = 3 * dims
+    packed_slot = packed[at : at + 1] + packed[at + 1 : at + 2] + packed[at + 2 : at + 3] - 1.0
+    target_slot = jnp.broadcast_to(packed_slot, (LANES, span)).T
+    lane = lax.broadcasted_iota(jnp.int32, (span, LANES), 1).astype(F32)
+    for at in range(0, shard_len, LANES):
+        placing[:, at : at + LANES] = jnp.where(lane + at == target_slot, 1.0, 0.0).astype(BF16)
+    height = (3 * walk_count + 7) // 8 * 8
+    row = lax.broadcasted_iota(jnp.int32, (height, span), 0)
+    own = jnp.zeros((height, span), jnp.bool_)
+    for index in range(walk_count):
+        own = own | (of_walk(index, height) & (row >= 3 * index) & (row < 3 * index + 3))
+    packed_squares = packed_walkers * packed_walkers
 
     def finish(total):
         live_total = total[dims + 1 : dims + 2]
@@ -397,19 +416,20 @@
         bias_ref[:, part] = biased(density)
         force_ref[:, part] = shared[chunk, 0:dims, :]
     density_sum = jnp.zeros((1, 1), F32)
-    merged = None
+    line = lax.broadcasted_iota(jnp.int32, (height, walk_len), 0)
+    lines = jnp.zeros((height, walk_len), F32)
     for index in range(walk_count):
         whole = jnp.concatenate([far[index, chunk] for chunk in range(owners)], 1)
         density_sum = density_sum + jnp.sum(whole, 1, keepdims=True)
-        packed = pack(row_of(split(whole), walk_len), index)
-        weight = jnp.exp(biased(packed[0:1] + packed[1:2] + packed[2:3]))
-        lin = split(weight * packed_walkers[index])
-        sq = split(weight * (packed_walkers[index] * packed_walkers[index]))
-        last = row_of(split(weight), capacity)
-        pad = jnp.zeros((8, capacity), F32)
-        feat = jnp.concatenate([lin[0], sq[0], lin[1], sq[1], lin[2], sq[2], last, pad], 0).astype(BF16)
-        add = lax.dot_general(feat, placing[index], (((1,), (1,)), ((), ())), preferred_element_type=F32)
-        merged = add if merged is None else merged + add
+        for part, value in enumerate(split(whole)):
+            lines = jnp.where(line == 3 * index + part, value, lines)
+    weight = jnp.exp(biased(jnp.sum(jnp.where(own, pack(lines), 0.0), 0, keepdims=True)))
+    lin = split(weight * packed_walkers)
+    sq = split(weight * packed_squares)
+    last = row_of(split(weight), span)
+    pad = jnp.zeros((8, span), F32)
+    feat = jnp.concatenate([lin[0], sq[0], lin[1], sq[1], lin[2], sq[2], last, pad], 0).astype(BF16)
+    merged = jnp.dot(feat, placing[...], preferred_element_type=F32)
     log_norm = jnp.log((1.0 - RATE) * norm + RATE * density_sum / (walk_len * walk_count))
     bias_ref[:, walk_len : walk_len + LANES] = jnp.broadcast_to(log_norm, (1, LANES))
 
@@ -426,10 +446,11 @@
     shift = first - centers * gain
     spread = second - 2.0 * centers * first + centers * centers * gain + new_sigma * new_sigma * gain
     new_heights = heights + gain
-    delta = shift / new_heights
+    inverse = 1.0 / new_heights
+    delta = shift * inverse
     new_heights_ref[...] = new_heights
     new_centers_ref[...] = centers + delta
-    new_sigmas_ref[...] = jnp.sqrt((heights * sigmas * sigmas + spread) / new_heights - delta * delta)
+    new_sigmas_ref[...] = jnp.sqrt((heights * sigmas * sigmas + spread) * inverse - delta * delta)
 
     always = walker_rows + (owners - 1) * rows
 
@@ -516,8 +537,8 @@
             pltpu.VMEM((walk_count, owners, 1, LANES), F32),
             pltpu.VMEM((walk_count, dims, walk_len), F32),
             pltpu.VMEM((walk_count, 1, walk_len), jnp.int32),
-            pltpu.VMEM((walk_count, capacity, walk_len), BF16),
-            pltpu.VMEM((walk_count, shard_len, capacity), BF16),
+            pltpu.VMEM((walk_len, walk_count * capacity), BF16),
+            pltpu.VMEM((walk_count * capacity, shard_len), BF16),
             pltpu.VMEM((spare_rows, LANES), F32),
             dma, dma((2,)), dma, dma, dma, dma,
         ],

time: 17.5 us -> 17.3 us (0.989)
  Pallas kernels: 15.4 us -> 15.2 us
where the time goes in v5:
time: 17.3 us; the launch traced here: 17.1 us
  Pallas kernels  15.2 us (88%)
  between operations  1.93 us (11%)
    pallas_call x1, Pallas kernels, per_device(): pl.pallas_call(functools.partial(sums_kernel, kern_count, walk_count, own...  14.5 us
    pallas_call x1, Pallas kernels, per_device(): pl.pallas_call(write_kernel, out_shape=[jax.ShapeDtypeStruct(shape, F32)...  0.72 us

profile of v5, /device:TPU:3, one launch (start us, length us, event | category | flops | bytes accessed | tf_op | source)
XLA Modules:
  0.0 17.1 jit_solution(6261513943807520333)
XLA Ops:
  1.9 14.5 %sums.1 = (f32[1,1152]{1,0:T(1,128)S(1)}, f32[8,1024]{1,0:T(8,128)S(1)}, f32[1,2048]{1,0:T(1,128)S(1)}, f32[8,2048]{1,0:T(8,128)S(1)}, f32[8,2048]{1,0:T(8,128)S(1)}) custom-call(f32[8,1024]{1,0:T(8,128)} %walkers_hbm.1, s32[1,1024]{1,0:T(1,128)} %bitcast.7, f32[8,2048]{1,0:T(8,128)} %centers_hbm.1, f32[8,2048]{1,0:T(8,128)} %sigmas_hbm.1, ...), custom_call_target="tpu_custom_call" | custom-call | tf_op jit(solution)/shard_map/sums/pallas_call | solution.py:511
  16.4 0.7 %write.1 = (f32[1,1024]{1,0:T(1,128)}, f32[8,1024]{1,0:T(8,128)}, f32[1,2048]{1,0:T(1,128)}, f32[8,2048]{1,0:T(8,128)}, f32[8,2048]{1,0:T(8,128)}, /*index=5*/f32[1,1]{1,0:T(1,128)}) custom-call(f32[1,1152]{1,0:T(1,128)S(1)} %get-tuple-element.17.bias_ref, f32[8,1024]{1,0:T(8,128)S(1)} %get-tuple-element.18.force_ref, ...), custom_call_target="tpu_custom_call" | custom-call | tf_op jit(solution)/shard_map/write/pallas_call | solution.py:552

commit v6 on v5

--- a/solution.py
+++ b/solution.py
@@ -42,9 +42,9 @@
                 walkers_hbm, target_hbm, centers_hbm, sigmas_hbm, heights_hbm, live_hbm, norm_hbm, new_sigma_hbm,
                 bias_ref, force_ref, new_heights_ref, new_centers_ref, new_sigmas_ref,
                 walkers_ref, target_ref, centers_ref, sigmas_ref, heights_ref, live_ref, norm_ref, new_sigma_ref, load_sem,
-                walker_feat, kernel_feat, kernel_mom, sums, got, early, early_got, early_far, direct, direct_far,
+                walker_feat, kernel_feat, kernel_mom, sums, got, direct, direct_far,
                 mine, shared, far, far_walkers, far_targets, table, placing, spare,
-                sent, recv_a, recv_d, recv_e, recv_b, recv_w):
+                sent, recv_a, recv_d, recv_b, recv_w):
     def load(source, target, index):
         return pltpu.make_async_copy(source, target, load_sem.at[index])
 
@@ -60,14 +60,27 @@
         copy.start()
     dims, walk_len = walkers_ref.shape
     shard_len = centers_ref.shape[1]
-    late = kern_count - owners
     rows = dims + 2
-    tail = owners - 2 * DIRECT
-    tails = owners - tail
     me = lax.axis_index("kern")
     walk = lax.axis_index("walk")
     flat = me * walk_count + walk
     total_count = kern_count * walk_count
+    quarters = owners // 2
+    head = quarters - DIRECT
+    half = quarters // 2
+    holders = [quarter + 1 for quarter in range(half)] + [
+        kern_count - 1 - (quarter + 1 - half) * (kern_count // quarters) for quarter in range(half, quarters)
+    ]
+    mine_quarter = 0
+    for quarter in range(1, quarters):
+        mine_quarter = jnp.where(me == holders[quarter], quarter, mine_quarter)
+    owns = me == holders[0]
+    for holder in holders[1:]:
+        owns = owns | (me == holder)
+    owns_head = owns & (mine_quarter < head)
+    owns_tail = owns & (mine_quarter >= head)
+    greets = owns | (me == 0)
+    greeted = (quarters + 1) * walk_count
 
     others = walk_count - 1
     load_rows = (dims * (walk_len + 2 * shard_len) + shard_len + walk_len) // LANES
@@ -89,7 +102,7 @@
             barrier, inc=1, device_id=(peer // walk_count, lax.rem(peer, walk_count)), device_id_type=MESH
         )
 
-    @pl.when(me < owners)
+    @pl.when(greets)
     def _():
         def greet_all(step, carry):
             greet(lax.rem(flat + step, total_count))
@@ -97,7 +110,7 @@
 
         lax.fori_loop(1, total_count, greet_all, 0)
 
-    @pl.when(me >= owners)
+    @pl.when(jnp.logical_not(greets))
     def _():
         for step in range(1, walk_count):
             greet(me * walk_count + other(step))
@@ -115,7 +128,6 @@
     stacked = jnp.concatenate(h + m + h + m + l + h + [row_of([one] * 3, walk_len), pad], 0)
     stacked = stacked.astype(BF16)
     width = 2 * LANES
-    quarters = walk_len // width
     for quarter in range(quarters):
         walker_feat[quarter] = stacked[:, quarter * width : (quarter + 1) * width]
 
@@ -142,51 +154,40 @@
     live_row = jnp.full((1, LANES), live, jnp.int32).astype(F32)
     block = min(512, shard_len)
 
-    def copy_a(owner, source):
+    def owner_of(quarter):
+        return holders[quarter]
+
+    def copy_a(quarter):
         return pltpu.make_async_remote_copy(
-            src_ref=sums.at[owner], dst_ref=got.at[source],
-            send_sem=sent, recv_sem=recv_a.at[0 if owner < tail else jnp.where((me > 0) & (me < owners), 0, 1)],
-            device_id=(owner, walk), device_id_type=MESH,
-        )
-
-    def copy_d(chunk):
+            src_ref=sums.at[quarter], dst_ref=got.at[me],
+            send_sem=sent, recv_sem=recv_a,
+            device_id=(owner_of(quarter), walk), device_id_type=MESH,
+        )
+
+    def copy_d(quarter):
         return pltpu.make_async_remote_copy(
-            src_ref=sums.at[pl.ds(chunk, 2)], dst_ref=direct.at[me - owners, pl.ds(chunk - tail, 2)],
+            src_ref=sums.at[quarter], dst_ref=direct.at[me - 1, quarter - head],
             send_sem=sent, recv_sem=recv_d,
             device_id=(0, walk), device_id_type=MESH,
         )
 
-    def copy_g(step, slot, chunk):
+    def copy_g(step, slot, quarter):
         return pltpu.make_async_remote_copy(
-            src_ref=sums.at[pl.ds(chunk, 2), pl.ds(dims, 1)], dst_ref=direct_far.at[walk, slot, pl.ds(chunk - tail, 2)],
+            src_ref=sums.at[quarter, :, pl.ds(dims, 1)], dst_ref=direct_far.at[walk, slot, quarter - head],
             send_sem=sent, recv_sem=recv_d,
             device_id=(0, other(step)), device_id_type=MESH,
         )
 
-    def copy_e():
+    def copy_b(target):
         return pltpu.make_async_remote_copy(
-            src_ref=early, dst_ref=early_got.at[me - tail],
-            send_sem=sent, recv_sem=recv_e,
-            device_id=(0, walk), device_id_type=MESH,
-        )
-
-    def copy_h(step):
-        return pltpu.make_async_remote_copy(
-            src_ref=early.at[pl.ds(dims, 1)], dst_ref=early_far.at[walk, me - tail],
-            send_sem=sent, recv_sem=recv_e,
-            device_id=(0, other(step)), device_id_type=MESH,
-        )
-
-    def copy_b(target, source):
-        return pltpu.make_async_remote_copy(
-            src_ref=mine, dst_ref=shared.at[source],
+            src_ref=mine, dst_ref=shared.at[mine_quarter],
             send_sem=sent, recv_sem=recv_b,
             device_id=(target, walk), device_id_type=MESH,
         )
 
-    def copy_c(step, target, source, origin):
+    def copy_c(step, target):
         return pltpu.make_async_remote_copy(
-            src_ref=mine.at[pl.ds(dims, 1)], dst_ref=far.at[origin, source],
+            src_ref=mine.at[:, pl.ds(dims, 1)], dst_ref=far.at[walk, mine_quarter],
             send_sem=sent, recv_sem=recv_b,
             device_id=(target, other(step)), device_id_type=MESH,
         )
@@ -224,30 +225,35 @@
         grad = c_sum - walkers_ref[:, quarter * width : (quarter + 1) * width] * a_sum
         for chunk in range(2):
             part = slice(chunk * LANES, (chunk + 1) * LANES)
-            sums[quarter * 2 + chunk, 0:dims, :] = grad[:, part]
-            sums[quarter * 2 + chunk, dims : dims + 1, :] = density[:, part]
-            sums[quarter * 2 + chunk, dims + 1 : dims + 2, :] = live_row
-
-    def sends_a(owner):
-        return me != owner
+            sums[quarter, chunk, 0:dims, :] = grad[:, part]
+            sums[quarter, chunk, dims : dims + 1, :] = density[:, part]
+            sums[quarter, chunk, dims + 1 : dims + 2, :] = live_row
 
     def send(quarter):
-        if 2 * quarter >= tail:
-            @pl.when(me >= owners)
+        if quarter >= head:
+            @pl.when(me > 0)
             def _():
-                copy_d(2 * quarter).start()
+                copy_d(quarter).start()
                 for step in range(1, walk_count):
-                    copy_g(step, me - owners, 2 * quarter).start()
+                    copy_g(step, me - 1, quarter).start()
 
             @pl.when(me == 0)
             def _():
                 for step in range(1, walk_count):
-                    copy_g(step, late, 2 * quarter).start()
-
-        for owner in (2 * quarter, 2 * quarter + 1):
-            @pl.when(sends_a(owner))
-            def _():
-                copy_a(owner, me).start()
+                    copy_g(step, kern_count - 1, quarter).start()
+
+        @pl.when(me != owner_of(quarter))
+        def _():
+            copy_a(quarter).start()
+
+    def enter():
+        @pl.when(greets)
+        def _():
+            pl.semaphore_wait(barrier, greeted - 1)
+
+        @pl.when(jnp.logical_not(greets))
+        def _():
+            pl.semaphore_wait(barrier, greeted + others)
 
     begin = 0
     for end in (quarters // 2, quarters):
@@ -257,7 +263,7 @@
         @pl.when(me >= owners)
         def _():
             if begin == 0:
-                pl.semaphore_wait(barrier, owners * walk_count + others)
+                enter()
             for quarter in range(begin, end):
                 send(quarter)
 
@@ -265,7 +271,7 @@
 
     @pl.when(me < owners)
     def _():
-        pl.semaphore_wait(barrier, owners * walk_count - 1)
+        enter()
         for quarter in range(quarters):
             send(quarter)
 
@@ -336,90 +342,75 @@
         return density, -PREFACTOR * (total[0:dims] / live_total) / (norm * ratio)
 
     def publish(total, begin):
-        density, force = finish(total)
-        mine[0:dims, :] = force
-        mine[dims : dims + 1, :] = density
+        for chunk in range(2):
+            density, force = finish(total[chunk])
+            mine[chunk, 0:dims, :] = force
+            mine[chunk, dims : dims + 1, :] = density
+            shared[mine_quarter, chunk, 0:dims, :] = force
+            shared[mine_quarter, chunk, dims : dims + 1, :] = density
 
         def start_b(target, carry):
             @pl.when(target != me)
             def _():
-                copy_b(target, me).start()
+                copy_b(target).start()
 
             for step in range(1, walk_count):
-                copy_c(step, target, me, walk).start()
+                copy_c(step, target).start()
             return carry
 
         lax.fori_loop(begin, kern_count, start_b, 0)
-        shared[me, 0:dims, :] = force
-        shared[me, dims : dims + 1, :] = density
-
-    @pl.when(me < tail)
-    def _():
-        got[me] = sums[me]
-        bulk((kern_count - 1) * rows, recv_a.at[0]).wait_recv()
+
+    @pl.when(owns_head | owns_tail)
+    def _():
+        got[me] = sums[mine_quarter]
+        bulk((kern_count - 1) * 2 * rows, recv_a).wait_recv()
         total = got[0]
         for source in range(1, kern_count):
             total = total + got[source]
-        publish(total, 0)
-
-    @pl.when((me >= tail) & (me < owners))
-    def _():
-        got[me] = sums[me]
-        bulk((owners - 2) * rows, recv_a.at[0]).wait_recv()
-        total = got[1]
-        for source in range(2, owners):
-            total = total + got[source]
-        early[...] = total
-        copy_e().start()
-        for step in range(1, walk_count):
-            copy_h(step).start()
-        bulk((late + 1) * rows, recv_a.at[1]).wait_recv()
-        whole = total + got[0]
-        for source in range(owners, kern_count):
-            whole = whole + got[source]
-        publish(whole, 1)
+        publish(total, jnp.where(owns_head, 0, 1))
 
     @pl.when(me == 0)
     def _():
-        bulk((tail - 1) * (dims + 1) + others * tail, recv_b).wait_recv()
-        bulk(tails * (rows + others), recv_e).wait_recv()
-        bulk(tails * (late * (rows + others) + others), recv_d).wait_recv()
-        for index in range(tails):
-            whole = early_got[index] + sums[tail + index]
-            for source in range(late):
+        bulk(head * 2 * (dims + 1 + others), recv_b).wait_recv()
+        bulk(DIRECT * 2 * ((kern_count - 1) * (rows + others) + others), recv_d).wait_recv()
+        for index in range(DIRECT):
+            whole = sums[head + index]
+            for source in range(kern_count - 1):
                 whole = whole + direct[source, index]
-            density, force = finish(whole)
-            shared[tail + index, 0:dims, :] = force
-            shared[tail + index, dims : dims + 1, :] = density
+            for chunk in range(2):
+                density, force = finish(whole[chunk])
+                shared[head + index, chunk, 0:dims, :] = force
+                shared[head + index, chunk, dims : dims + 1, :] = density
             for step in range(1, walk_count):
                 origin = other(step)
-                distant = early_far[origin, index]
-                for source in range(late + 1):
+                distant = direct_far[origin, 0, index]
+                for source in range(1, kern_count):
                     distant = distant + direct_far[origin, source, index]
-                far[origin, tail + index] = distant / whole[dims + 1 : dims + 2]
-
-    @pl.when((me > 0) & (me < owners))
-    def _():
-        bulk((owners - 1) * (dims + 1) + others * owners, recv_b).wait_recv()
-
-    @pl.when(me >= owners)
-    def _():
-        bulk(owners * (dims + 1) + others * owners, recv_b).wait_recv()
+                for chunk in range(2):
+                    far[origin, head + index, chunk] = distant[chunk] / whole[chunk, dims + 1 : dims + 2]
+
+    @pl.when(owns_head | owns_tail)
+    def _():
+        bulk(2 * ((quarters - 1) * (dims + 1) + others * quarters), recv_b).wait_recv()
+
+    @pl.when((me > 0) & jnp.logical_not(owns_head | owns_tail))
+    def _():
+        bulk(2 * (quarters * (dims + 1) + others * quarters), recv_b).wait_recv()
 
     def biased(density):
         return PREFACTOR * jnp.log(density / norm + EPSILON)
 
     for chunk in range(owners):
         part = slice(chunk * LANES, (chunk + 1) * LANES)
-        density = shared[chunk, dims : dims + 1, :]
-        far[walk, chunk] = density
+        density = shared[chunk // 2, chunk % 2, dims : dims + 1, :]
+        far[walk, chunk // 2, chunk % 2] = density
         bias_ref[:, part] = biased(density)
-        force_ref[:, part] = shared[chunk, 0:dims, :]
+        force_ref[:, part] = shared[chunk // 2, chunk % 2, 0:dims, :]
     density_sum = jnp.zeros((1, 1), F32)
     line = lax.broadcasted_iota(jnp.int32, (height, walk_len), 0)
     lines = jnp.zeros((height, walk_len), F32)
     for index in range(walk_count):
-        whole = jnp.concatenate([far[index, chunk] for chunk in range(owners)], 1)
+        whole = jnp.concatenate([far[index, chunk // 2, chunk % 2] for chunk in range(owners)], 1)
         density_sum = density_sum + jnp.sum(whole, 1, keepdims=True)
         for part, value in enumerate(split(whole)):
             lines = jnp.where(line == 3 * index + part, value, lines)
@@ -452,23 +443,24 @@
     new_centers_ref[...] = centers + delta
     new_sigmas_ref[...] = jnp.sqrt((heights * sigmas * sigmas + spread) * inverse - delta * delta)
 
-    always = walker_rows + (owners - 1) * rows
-
-    @pl.when(me >= owners)
-    def _():
-        bulk(always + rows + tails * (rows + others), sent).wait_send()
-
-    @pl.when((me > 0) & (me < tail))
-    def _():
-        bulk(always + (kern_count - 1) * (dims + 1) + others * kern_count, sent).wait_send()
+    always = walker_rows + (quarters - 1) * 2 * rows
+    direct_rows = DIRECT * 2 * (rows + others)
+
+    @pl.when(owns_head)
+    def _():
+        bulk(always + direct_rows + 2 * ((kern_count - 1) * (dims + 1) + others * kern_count), sent).wait_send()
+
+    @pl.when(owns_tail)
+    def _():
+        bulk(always + direct_rows + 2 * ((kern_count - 2) * (dims + 1) + others * (kern_count - 1)), sent).wait_send()
 
     @pl.when(me == 0)
     def _():
-        bulk(always + (kern_count - 1) * (dims + 1) + others * (kern_count + tails), sent).wait_send()
-
-    @pl.when((me >= tail) & (me < owners))
-    def _():
-        bulk(always + rows + (kern_count - 2) * (dims + 1) + others * kern_count, sent).wait_send()
+        bulk(always + 2 * rows + DIRECT * 2 * others, sent).wait_send()
+
+    @pl.when((me > 0) & jnp.logical_not(owns_head | owns_tail))
+    def _():
+        bulk(always + 2 * rows + direct_rows, sent).wait_send()
 
 
 def write_kernel(bias_ref, force_ref, new_heights_ref, new_centers_ref, new_sigmas_ref,
@@ -496,14 +488,13 @@
     kern_count = lax.axis_size("kern")
     walk_count = lax.axis_size("walk")
     owners = walk_len // LANES
-    late = kern_count - owners
     quarters = owners // 2
     rows = dims + 2
     capacity = 2 * walk_len // kern_count
     height_row = heights.reshape(1, shard_len)
     load_rows = (dims * (walk_len + 2 * shard_len) + shard_len + walk_len) // LANES
     walker_rows = walk_count * (dims + 1) * walk_len // LANES
-    answer_rows = walk_count * kern_count + kern_count * rows
+    answer_rows = 2 * kern_count * (walk_count + rows)
     spare_rows = load_rows + walker_rows + answer_rows + kern_count * owners * (rows + walk_count)
 
     dma = pltpu.SemaphoreType.DMA
@@ -525,22 +516,19 @@
             pltpu.VMEM((walk_len // (2 * LANES), LANES, 2 * LANES), BF16),
             pltpu.VMEM((shard_len, LANES), BF16),
             pltpu.VMEM((6 * dims + 16, shard_len), BF16),
-            pltpu.VMEM((owners, rows, LANES), F32),
-            pltpu.VMEM((kern_count, rows, LANES), F32),
-            pltpu.VMEM((rows, LANES), F32),
-            pltpu.VMEM((2 * DIRECT, rows, LANES), F32),
-            pltpu.VMEM((walk_count, 2 * DIRECT, 1, LANES), F32),
-            pltpu.VMEM((late, 2 * DIRECT, rows, LANES), F32),
-            pltpu.VMEM((walk_count, late + 1, 2 * DIRECT, 1, LANES), F32),
-            pltpu.VMEM((dims + 1, LANES), F32),
-            pltpu.VMEM((owners, dims + 1, LANES), F32),
-            pltpu.VMEM((walk_count, owners, 1, LANES), F32),
+            pltpu.VMEM((quarters, 2, rows, LANES), F32),
+            pltpu.VMEM((kern_count, 2, rows, LANES), F32),
+            pltpu.VMEM((kern_count - 1, DIRECT, 2, rows, LANES), F32),
+            pltpu.VMEM((walk_count, kern_count, DIRECT, 2, 1, LANES), F32),
+            pltpu.VMEM((2, dims + 1, LANES), F32),
+            pltpu.VMEM((quarters, 2, dims + 1, LANES), F32),
+            pltpu.VMEM((walk_count, quarters, 2, 1, LANES), F32),
             pltpu.VMEM((walk_count, dims, walk_len), F32),
             pltpu.VMEM((walk_count, 1, walk_len), jnp.int32),
             pltpu.VMEM((walk_len, walk_count * capacity), BF16),
             pltpu.VMEM((walk_count * capacity, shard_len), BF16),
             pltpu.VMEM((spare_rows, LANES), F32),
-            dma, dma((2,)), dma, dma, dma, dma,
+            dma, dma, dma, dma, dma,
         ],
         compiler_params=pltpu.CompilerParams(collective_id=0, has_side_effects=True, vmem_limit_bytes=LIMIT),
         name="sums",

time: 17.3 us -> 17 us (0.983)
  the two profiles are of different devices: /device:TPU:3 before, /device:TPU:0 now
where the time goes in v6:
time: 17 us; the launch traced here: 16.8 us
  Pallas kernels  14.9 us (88%)
  between operations  1.93 us (11%)
    pallas_call x1, Pallas kernels, per_device(): pl.pallas_call(functools.partial(sums_kernel, kern_count, walk_count, own...  14.2 us
    pallas_call x1, Pallas kernels, per_device(): pl.pallas_call(write_kernel, out_shape=[jax.ShapeDtypeStruct(shape, F32)...  0.72 us

profile of v6, /device:TPU:0, one launch (start us, length us, event | category | flops | bytes accessed | tf_op | source)
XLA Modules:
  0.0 16.8 jit_solution(2487530516858474011)
XLA Ops:
  1.9 14.2 %sums.1 = (f32[1,1152]{1,0:T(1,128)S(1)}, f32[8,1024]{1,0:T(8,128)S(1)}, f32[1,2048]{1,0:T(1,128)S(1)}, f32[8,2048]{1,0:T(8,128)S(1)}, f32[8,2048]{1,0:T(8,128)S(1)}) custom-call(f32[8,1024]{1,0:T(8,128)} %walkers_hbm.1, s32[1,1024]{1,0:T(1,128)} %bitcast.7, f32[8,2048]{1,0:T(8,128)} %centers_hbm.1, f32[8,2048]{1,0:T(8,128)} %sigmas_hbm.1, ...), custom_call_target="tpu_custom_call" | custom-call | tf_op jit(solution)/shard_map/sums/pallas_call | solution.py:502
  16.1 0.7 %write.1 = (f32[1,1024]{1,0:T(1,128)}, f32[8,1024]{1,0:T(8,128)}, f32[1,2048]{1,0:T(1,128)}, f32[8,2048]{1,0:T(8,128)}, f32[8,2048]{1,0:T(8,128)}, /*index=5*/f32[1,1]{1,0:T(1,128)}) custom-call(f32[1,1152]{1,0:T(1,128)S(1)} %get-tuple-element.17.bias_ref, f32[8,1024]{1,0:T(8,128)S(1)} %get-tuple-element.18.force_ref, ...), custom_call_target="tpu_custom_call" | custom-call | tf_op jit(solution)/shard_map/write/pallas_call | solution.py:540

commit v7 on v6

--- a/solution.py
+++ b/solution.py
@@ -371,7 +371,6 @@
 
     @pl.when(me == 0)
     def _():
-        bulk(head * 2 * (dims + 1 + others), recv_b).wait_recv()
         bulk(DIRECT * 2 * ((kern_count - 1) * (rows + others) + others), recv_d).wait_recv()
         for index in range(DIRECT):
             whole = sums[head + index]
@@ -388,6 +387,7 @@
                     distant = distant + direct_far[origin, source, index]
                 for chunk in range(2):
                     far[origin, head + index, chunk] = distant[chunk] / whole[chunk, dims + 1 : dims + 2]
+        bulk(head * 2 * (dims + 1 + others), recv_b).wait_recv()
 
     @pl.when(owns_head | owns_tail)
     def _():

time: 17 us -> 16.9 us (level)
  no operation moved by 1% of the time
where the time goes in v7:
time: 16.9 us; the launch traced here: 16.8 us
  Pallas kernels  14.8 us (88%)
  between operations  1.93 us (11%)
    pallas_call x1, Pallas kernels, per_device(): pl.pallas_call(functools.partial(sums_kernel, kern_count, walk_count, own...  14.1 us
    pallas_call x1, Pallas kernels, per_device(): pl.pallas_call(write_kernel, out_shape=[jax.ShapeDtypeStruct(shape, F32)...  0.72 us

profile of v7, /device:TPU:0, one launch (start us, length us, event | category | flops | bytes accessed | tf_op | source)
XLA Modules:
  0.0 16.8 jit_solution(13388875384141333087)
XLA Ops:
  1.9 14.1 %sums.1 = (f32[1,1152]{1,0:T(1,128)S(1)}, f32[8,1024]{1,0:T(8,128)S(1)}, f32[1,2048]{1,0:T(1,128)S(1)}, f32[8,2048]{1,0:T(8,128)S(1)}, f32[8,2048]{1,0:T(8,128)S(1)}) custom-call(f32[8,1024]{1,0:T(8,128)} %walkers_hbm.1, s32[1,1024]{1,0:T(1,128)} %bitcast.7, f32[8,2048]{1,0:T(8,128)} %centers_hbm.1, f32[8,2048]{1,0:T(8,128)} %sigmas_hbm.1, ...), custom_call_target="tpu_custom_call" | custom-call | tf_op jit(solution)/shard_map/sums/pallas_call | solution.py:502
  16.0 0.7 %write.1 = (f32[1,1024]{1,0:T(1,128)}, f32[8,1024]{1,0:T(8,128)}, f32[1,2048]{1,0:T(1,128)}, f32[8,2048]{1,0:T(8,128)}, f32[8,2048]{1,0:T(8,128)}, /*index=5*/f32[1,1]{1,0:T(1,128)}) custom-call(f32[1,1152]{1,0:T(1,128)S(1)} %get-tuple-element.17.bias_ref, f32[8,1024]{1,0:T(8,128)S(1)} %get-tuple-element.18.force_ref, ...), custom_call_target="tpu_custom_call" | custom-call | tf_op jit(solution)/shard_map/write/pallas_call | solution.py:540

commit v8 on v7

--- a/solution.py
+++ b/solution.py
@@ -464,7 +464,7 @@
 
 
 def write_kernel(bias_ref, force_ref, new_heights_ref, new_centers_ref, new_sigmas_ref,
-                 bias_hbm, force_hbm, new_heights_hbm, new_centers_hbm, new_sigmas_hbm, log_norm_hbm, log_norm_ref, sem):
+                 bias_hbm, force_hbm, new_heights_hbm, new_centers_hbm, new_sigmas_hbm, log_norm_hbm, log_norm_ref, spare, sem):
     walk_len = bias_hbm.shape[1]
     log_norm_ref[...] = bias_ref[:, walk_len : walk_len + 1]
     pairs = [
@@ -475,11 +475,11 @@
         (bias_ref.at[:, pl.ds(0, walk_len)], bias_hbm),
         (log_norm_ref, log_norm_hbm),
     ]
-    copies = [pltpu.make_async_copy(source, target, sem.at[index]) for index, (source, target) in enumerate(pairs)]
+    copies = [pltpu.make_async_copy(source, target, sem.at[index // 5]) for index, (source, target) in enumerate(pairs)]
     for copy in copies:
         copy.start()
-    for copy in copies:
-        copy.wait()
+    pltpu.make_async_copy(spare, spare, sem.at[0]).wait()
+    copies[5].wait()
 
 
 def per_device(walkers, centers, sigmas, heights, kernel_live, merge_target, new_sigma, norm_old):
@@ -542,7 +542,7 @@
         out_shape=[jax.ShapeDtypeStruct(shape, F32) for shape in shapes],
         in_specs=[VMEM] * 5,
         out_specs=[HBM] * 6,
-        scratch_shapes=[pltpu.VMEM((1, 1), F32), dma((6,))],
+        scratch_shapes=[pltpu.VMEM((1, 1), F32), pltpu.VMEM((load_rows, LANES), F32), dma((2,))],
         compiler_params=pltpu.CompilerParams(vmem_limit_bytes=LIMIT),
         name="write",
     )(*results)

time: 16.9 us -> 16.9 us (level)
  no operation moved by 1% of the time
where the time goes in v8:
time: 16.9 us; the launch traced here: 16.7 us
  Pallas kernels  14.8 us (88%)
  between operations  1.93 us (11%)
    pallas_call x1, Pallas kernels, per_device(): pl.pallas_call(functools.partial(sums_kernel, kern_count, walk_count, own...  14.1 us
    pallas_call x1, Pallas kernels, per_device(): pl.pallas_call(write_kernel, out_shape=[jax.ShapeDtypeStruct(shape, F32)...  0.68 us

profile of v8, /device:TPU:0, one launch (start us, length us, event | category | flops | bytes accessed | tf_op | source)
XLA Modules:
  0.0 16.7 jit_solution(8737246924085345463)
XLA Ops:
  1.9 14.1 %sums.1 = (f32[1,1152]{1,0:T(1,128)S(1)}, f32[8,1024]{1,0:T(8,128)S(1)}, f32[1,2048]{1,0:T(1,128)S(1)}, f32[8,2048]{1,0:T(8,128)S(1)}, f32[8,2048]{1,0:T(8,128)S(1)}) custom-call(f32[8,1024]{1,0:T(8,128)} %walkers_hbm.1, s32[1,1024]{1,0:T(1,128)} %bitcast.7, f32[8,2048]{1,0:T(8,128)} %centers_hbm.1, f32[8,2048]{1,0:T(8,128)} %sigmas_hbm.1, ...), custom_call_target="tpu_custom_call" | custom-call | tf_op jit(solution)/shard_map/sums/pallas_call | solution.py:502
  16.0 0.7 %write.1 = (f32[1,1024]{1,0:T(1,128)}, f32[8,1024]{1,0:T(8,128)}, f32[1,2048]{1,0:T(1,128)}, f32[8,2048]{1,0:T(8,128)}, f32[8,2048]{1,0:T(8,128)}, /*index=5*/f32[1,1]{1,0:T(1,128)}) custom-call(f32[1,1152]{1,0:T(1,128)S(1)} %get-tuple-element.17.bias_ref, f32[8,1024]{1,0:T(8,128)S(1)} %get-tuple-element.18.force_ref, ...), custom_call_target="tpu_custom_call" | custom-call | tf_op jit(solution)/shard_map/write/pallas_call | solution.py:540
